TPU v7x, 64 devices: a 2x2x8 block of a 4x4x8 slice. The times are simulated.
64 devices in a mesh: data: 4 (over x, y), stage: 16 (over z, core).
Axes of the slice: x: 2, y: 2, z: 8, core: 2. Of those that a mesh axis runs over, the one named last changes fastest.
The devices are a block of a 4x4x8 slice.
Arguments:
- x_init: float32 [8, 256, 16], P('data'), parts along dimension 0
- h_warm: bfloat16 [15, 8, 256, 512], P(None, 'data'), parts along dimension 1
- skip_warm: bfloat16 [8, 8, 256, 512], P(None, 'data'), parts along dimension 1
- w_in: bfloat16 [16, 512], replicated
- w_out: bfloat16 [512, 16], replicated
- w_qkv: bfloat16 [16, 512, 1536], P('stage')
- w_o: bfloat16 [16, 8, 64, 512], P('stage')
- w_up: bfloat16 [16, 512, 2048], P('stage')
- w_down: bfloat16 [16, 2048, 512], P('stage')
- w_skip: bfloat16 [8, 1024, 512], replicated
- ada_mods: float32 [32, 16, 6, 512], P(None, 'stage')
- coef_keep: float32 [32], replicated
- coef_noise: float32 [32], replicated
Outputs:
- output: float32 [8, 256, 16], P('data'), parts along dimension 0
There are 4 independent parts. A program takes and returns all parts, laid end to end along the dimension named above; an argument that names none is the same for every part.
All inputs are finite; a program needn't handle non-finite values.
Results may differ from a plain program's by a relative error of at most 0.0126811.
Values are sent between devices in bfloat16 or wider.
A program may use at most 768 MiB of HBM per device.

v0:
```python
import jax
import jax.numpy as jnp
from jax import lax
from jax.sharding import PartitionSpec as P
import math


def layer_norm(hidden):
    centered = hidden - jnp.mean(hidden, axis=-1, keepdims=True)
    variance = jnp.mean(centered * centered, axis=-1, keepdims=True)
    return centered * lax.rsqrt(variance + 1e-6)


def value_a9(hidden, block_mod, wqkv_one, wo_one, wup_one, wdown_one):
    batch_size, tokens = hidden.shape[0], hidden.shape[1]
    num_heads, head_dim = wo_one.shape[0], wo_one.shape[1]
    normed = layer_norm(hidden) * (1.0 + block_mod[1]) + block_mod[0]
    qkv_all = jnp.einsum('btd,de->bte', normed.astype(jnp.bfloat16), wqkv_one, preferred_element_type=jnp.float32).astype(jnp.bfloat16)
    qkv_all = qkv_all.reshape(batch_size, tokens, 3, num_heads, head_dim)
    scores = jnp.einsum('bqhd,bkhd->bhqk', qkv_all[:, :, 0], qkv_all[:, :, 1], preferred_element_type=jnp.float32) * (1.0 / math.sqrt(head_dim))
    attn_probs = jax.nn.softmax(scores, axis=-1).astype(jnp.bfloat16)
    attended = jnp.einsum('bhqk,bkhd->bqhd', attn_probs, qkv_all[:, :, 2], preferred_element_type=jnp.float32).astype(jnp.bfloat16)
    attn_out = jnp.einsum('bqhd,hde->bqe', attended, wo_one, preferred_element_type=jnp.float32)
    hidden = hidden + block_mod[2] * attn_out
    normed = layer_norm(hidden) * (1.0 + block_mod[4]) + block_mod[3]
    mlp_hidden = jnp.einsum('btd,df->btf', normed.astype(jnp.bfloat16), wup_one, preferred_element_type=jnp.float32)
    gelu_act = jax.nn.gelu(mlp_hidden, approximate=True).astype(jnp.bfloat16)
    mlp_out = jnp.einsum('btf,fd->btd', gelu_act, wdown_one, preferred_element_type=jnp.float32)
    return hidden + block_mod[5] * mlp_out


def skip_project(hidden, skip_one, wskip_one):
    model_width = hidden.shape[-1]
    main_part = jnp.einsum('btd,de->bte', hidden.astype(jnp.bfloat16), wskip_one[:model_width], preferred_element_type=jnp.float32)
    skip_part = jnp.einsum('btd,de->bte', skip_one, wskip_one[model_width:], preferred_element_type=jnp.float32)
    return main_part + skip_part


def keep_hidden(hidden, skip_one, wskip_one):
    return hidden


def solution(mesh):
    stages = mesh.shape['stage']
    half_stages = stages // 2
    chain_perm = [(source, source + 1) for source in range(stages - 1)]
    mirror_perm = [(source, stages - 1 - source) for source in range(half_stages)]
    return_perm = [(stages - 1, 0)]

    def local_run(x_init, h_warm, skip_warm, w_in, w_out, w_qkv, w_o, w_up, w_down, w_skip, ada_mods, coef_keep, coef_noise):
        per_stage = w_qkv.shape[0]
        half_layers = w_skip.shape[0]
        stage_id = lax.axis_index('stage')
        is_second = stage_id >= half_stages
        bound_init = lax.dynamic_index_in_dim(h_warm, jnp.maximum(stage_id - 1, 0), 0, keepdims=False)
        mirror_start = jnp.minimum(stages - 1 - stage_id, half_stages - 1) * per_stage
        skip_init = lax.dynamic_slice_in_dim(skip_warm, mirror_start, per_stage, 0)

        def step_body(state_in, step_in):
            latent, bound_in, skip_in = state_in
            step_mods, keep_one, noise_one = step_in
            from_latent = jnp.einsum('btc,cd->btd', latent.astype(jnp.bfloat16), w_in, preferred_element_type=jnp.float32)
            hidden = jnp.where(stage_id == 0, from_latent, bound_in.astype(jnp.float32))
            block_outs = []
            for offset in range(per_stage):
                skip_id = jnp.maximum(stage_id * per_stage + offset - half_layers, 0)
                wskip_one = lax.dynamic_index_in_dim(w_skip, skip_id, 0, keepdims=False)
                hidden = lax.cond(is_second, skip_project, keep_hidden, hidden, skip_in[per_stage - 1 - offset], wskip_one)
                hidden = value_a9(hidden, step_mods[offset], w_qkv[offset], w_o[offset], w_up[offset], w_down[offset])
                block_outs.append(hidden.astype(jnp.bfloat16))
            stage_out = block_outs[-1]
            noise_pred = jnp.einsum('btd,dc->btc', stage_out, w_out, preferred_element_type=jnp.float32)
            new_latent = keep_one * latent + noise_one * noise_pred
            next_bound = lax.ppermute(stage_out, 'stage', chain_perm)
            next_skips = lax.ppermute(jnp.stack(block_outs), 'stage', mirror_perm)
            returned = lax.ppermute(new_latent, 'stage', return_perm)
            latent_next = jnp.where(stage_id == 0, returned, new_latent)
            return (latent_next, next_bound, next_skips), None

        final_state = lax.scan(step_body, (x_init, bound_init, skip_init), (ada_mods, coef_keep, coef_noise))[0]
        final_latent = final_state[0]
        return lax.psum(jnp.where(stage_id == stages - 1, final_latent, jnp.zeros_like(final_latent)), 'stage')

    in_specs = (P('data'), P(None, 'data'), P(None, 'data'), P(), P(), P('stage'), P('stage'), P('stage'), P('stage'), P(), P(None, 'stage'), P(), P())
    return jax.shard_map(local_run, mesh=mesh, in_specs=in_specs, out_specs=P('data'), check_vma=False)
```

profile of v0, /device:TPU:21, one launch (start us, length us, event | category | flops | bytes accessed | tf_op | source)
XLA Modules:
  0.0 1628.6 jit_solution(2058806768334034523)
XLA Ops:
  4.6 1579.0 %while.16 = (s32[]{:T(128)}, f32[2,256,16]{1,2,0:T(8,128)S(1)}, bf16[2,256,512]{2,1,0:T(8,128)(2,1)S(1)}, bf16[1,2,256,512]{3,2,1,0:T(8,128)(2,1)S(1)}, pred[]{:...) while((s32[]{:T(128)}, f32[2,256,16]{1,2,0:T(8,128)S(1)}, ...), condition=%wide.region_9.10_spmd, body=%wide.region_0.9_spmd.sunk | while | flops 4067207424 | bytes 49750504 | solution.py:80
  45.1 18.7 %collective-permute-done.2 = bf16[1,2,256,512]{3,2,1,0:T(8,128)(2,1)S(1)} collective-permute-done((bf16[1,2,256,512]{3,2,1,0:T(8,128)(2,1)S(1)}, bf16[1,2,256,512]{3,2,1,0:T(8,128)(2,1)S(1)}, u32[]{:S(2)}, u32[]{:S(2)}) %collective-permute-start.2) | collective-permute-done | bytes 524320 | tf_op jit(solution)/shard_map/while/body/eval_jaxpr/ppermute | solution.py:75
  148.4 13.4 collective-permute-done.2
  197.7 13.0 collective-permute-done.2
  246.6 13.3 collective-permute-done.2
  295.8 13.0 collective-permute-done.2
  344.7 13.3 collective-permute-done.2
  393.8 13.0 collective-permute-done.2
  442.7 13.3 collective-permute-done.2
  491.9 13.0 collective-permute-done.2
  540.8 13.3 collective-permute-done.2
  590.0 13.0 collective-permute-done.2
  638.9 13.3 collective-permute-done.2
  688.0 13.0 collective-permute-done.2
  736.9 13.3 collective-permute-done.2
  786.1 13.0 collective-permute-done.2
  835.0 13.3 collective-permute-done.2
  884.1 13.0 collective-permute-done.2
  933.0 13.3 collective-permute-done.2
  982.2 13.0 collective-permute-done.2
  1031.1 13.3 collective-permute-done.2
  1080.3 13.0 collective-permute-done.2
  1129.2 13.3 collective-permute-done.2
  1178.3 13.0 collective-permute-done.2
  1227.2 13.3 collective-permute-done.2
  1276.4 13.0 collective-permute-done.2
  1325.3 13.3 collective-permute-done.2
  1374.5 13.0 collective-permute-done.2
  1423.4 13.3 collective-permute-done.2
  1472.5 13.0 collective-permute-done.2
  1521.4 13.3 collective-permute-done.2
  1583.6 45.0 %psum.7 = f32[2,256,16]{1,2,0:T(8,128)} all-reduce(f32[2,256,16]{1,2,0:T(8,128)S(1)} %broadcast_select_fusion.1), channel_id=1, replica_groups=mesh['data'=4,'stage'=16] {'stage'}, use_global_device_ids=true, to_apply=%region_10.11 | all-reduce | flops 8192 | bytes 65536 | tf_op jit(solution)/shard_map/psum | solution.py:82
  (816 shorter events, 1180.2 us)
Async XLA Ops:
  31.5 32.3 %collective-permute-start.2 = (bf16[1,2,256,512]{3,2,1,0:T(8,128)(2,1)S(1)}, bf16[1,2,256,512]{3,2,1,0:T(8,128)(2,1)S(1)}, u32[]{:S(2)}, u32[]{:S(2)}) collective-permute-start(bf16[1,2,256,512]{3,2,1,0:T(8,128)(2,1)S(1)} %bitcast.129), channel_id=1, source_target_pairs={{0,15},{1,14},{2,13},{3,12},{4,11},{5,10},{6,9},{7,8},{16,31},{17,... | collective-permute-start | bytes 1572872 | tf_op jit(solution)/shard_map/while/body/eval_jaxpr/ppermute | solution.py:75
  87.5 25.0 %collective-permute-start.2 = (bf16[1,2,256,512]{3,2,1,0:T(8,128)(2,1)S(1)}, bf16[1,2,256,512]{3,2,1,0:T(8,128)(2,1)S(1)}, u32[]{:S(2)}, u32[]{:S(2)}) collective-permute-start(bf16[1,2,256,512]{3,2,1,0:T(8,128)(2,1)S(1)} %bitcast.129), channel_id=1, source_target_pairs={{0,15},{1,14},{2,13},{3,12},{4,11},{5,10},{6,9},{7,8},{16,31},{17,... | collective-permute-start | bytes 1572872 | tf_op jit(solution)/shard_map/while/body/eval_jaxpr/ppermute | solution.py:75
  136.3 25.5 %collective-permute-start.2 = (bf16[1,2,256,512]{3,2,1,0:T(8,128)(2,1)S(1)}, bf16[1,2,256,512]{3,2,1,0:T(8,128)(2,1)S(1)}, u32[]{:S(2)}, u32[]{:S(2)}) collective-permute-start(bf16[1,2,256,512]{3,2,1,0:T(8,128)(2,1)S(1)} %bitcast.129), channel_id=1, source_target_pairs={{0,15},{1,14},{2,13},{3,12},{4,11},{5,10},{6,9},{7,8},{16,31},{17,... | collective-permute-start | bytes 1572872 | tf_op jit(solution)/shard_map/while/body/eval_jaxpr/ppermute | solution.py:75
  185.6 25.1 %collective-permute-start.2 = (bf16[1,2,256,512]{3,2,1,0:T(8,128)(2,1)S(1)}, bf16[1,2,256,512]{3,2,1,0:T(8,128)(2,1)S(1)}, u32[]{:S(2)}, u32[]{:S(2)}) collective-permute-start(bf16[1,2,256,512]{3,2,1,0:T(8,128)(2,1)S(1)} %bitcast.129), channel_id=1, source_target_pairs={{0,15},{1,14},{2,13},{3,12},{4,11},{5,10},{6,9},{7,8},{16,31},{17,... | collective-permute-start | bytes 1572872 | tf_op jit(solution)/shard_map/while/body/eval_jaxpr/ppermute | solution.py:75
  234.5 25.4 %collective-permute-start.2 = (bf16[1,2,256,512]{3,2,1,0:T(8,128)(2,1)S(1)}, bf16[1,2,256,512]{3,2,1,0:T(8,128)(2,1)S(1)}, u32[]{:S(2)}, u32[]{:S(2)}) collective-permute-start(bf16[1,2,256,512]{3,2,1,0:T(8,128)(2,1)S(1)} %bitcast.129), channel_id=1, source_target_pairs={{0,15},{1,14},{2,13},{3,12},{4,11},{5,10},{6,9},{7,8},{16,31},{17,... | collective-permute-start | bytes 1572872 | tf_op jit(solution)/shard_map/while/body/eval_jaxpr/ppermute | solution.py:75
  283.6 25.1 %collective-permute-start.2 = (bf16[1,2,256,512]{3,2,1,0:T(8,128)(2,1)S(1)}, bf16[1,2,256,512]{3,2,1,0:T(8,128)(2,1)S(1)}, u32[]{:S(2)}, u32[]{:S(2)}) collective-permute-start(bf16[1,2,256,512]{3,2,1,0:T(8,128)(2,1)S(1)} %bitcast.129), channel_id=1, source_target_pairs={{0,15},{1,14},{2,13},{3,12},{4,11},{5,10},{6,9},{7,8},{16,31},{17,... | collective-permute-start | bytes 1572872 | tf_op jit(solution)/shard_map/while/body/eval_jaxpr/ppermute | solution.py:75
  332.5 25.4 %collective-permute-start.2 = (bf16[1,2,256,512]{3,2,1,0:T(8,128)(2,1)S(1)}, bf16[1,2,256,512]{3,2,1,0:T(8,128)(2,1)S(1)}, u32[]{:S(2)}, u32[]{:S(2)}) collective-permute-start(bf16[1,2,256,512]{3,2,1,0:T(8,128)(2,1)S(1)} %bitcast.129), channel_id=1, source_target_pairs={{0,15},{1,14},{2,13},{3,12},{4,11},{5,10},{6,9},{7,8},{16,31},{17,... | collective-permute-start | bytes 1572872 | tf_op jit(solution)/shard_map/while/body/eval_jaxpr/ppermute | solution.py:75
  381.7 25.1 %collective-permute-start.2 = (bf16[1,2,256,512]{3,2,1,0:T(8,128)(2,1)S(1)}, bf16[1,2,256,512]{3,2,1,0:T(8,128)(2,1)S(1)}, u32[]{:S(2)}, u32[]{:S(2)}) collective-permute-start(bf16[1,2,256,512]{3,2,1,0:T(8,128)(2,1)S(1)} %bitcast.129), channel_id=1, source_target_pairs={{0,15},{1,14},{2,13},{3,12},{4,11},{5,10},{6,9},{7,8},{16,31},{17,... | collective-permute-start | bytes 1572872 | tf_op jit(solution)/shard_map/while/body/eval_jaxpr/ppermute | solution.py:75
  430.6 25.4 %collective-permute-start.2 = (bf16[1,2,256,512]{3,2,1,0:T(8,128)(2,1)S(1)}, bf16[1,2,256,512]{3,2,1,0:T(8,128)(2,1)S(1)}, u32[]{:S(2)}, u32[]{:S(2)}) collective-permute-start(bf16[1,2,256,512]{3,2,1,0:T(8,128)(2,1)S(1)} %bitcast.129), channel_id=1, source_target_pairs={{0,15},{1,14},{2,13},{3,12},{4,11},{5,10},{6,9},{7,8},{16,31},{17,... | collective-permute-start | bytes 1572872 | tf_op jit(solution)/shard_map/while/body/eval_jaxpr/ppermute | solution.py:75
  479.8 25.1 %collective-permute-start.2 = (bf16[1,2,256,512]{3,2,1,0:T(8,128)(2,1)S(1)}, bf16[1,2,256,512]{3,2,1,0:T(8,128)(2,1)S(1)}, u32[]{:S(2)}, u32[]{:S(2)}) collective-permute-start(bf16[1,2,256,512]{3,2,1,0:T(8,128)(2,1)S(1)} %bitcast.129), channel_id=1, source_target_pairs={{0,15},{1,14},{2,13},{3,12},{4,11},{5,10},{6,9},{7,8},{16,31},{17,... | collective-permute-start | bytes 1572872 | tf_op jit(solution)/shard_map/while/body/eval_jaxpr/ppermute | solution.py:75
  528.6 25.4 %collective-permute-start.2 = (bf16[1,2,256,512]{3,2,1,0:T(8,128)(2,1)S(1)}, bf16[1,2,256,512]{3,2,1,0:T(8,128)(2,1)S(1)}, u32[]{:S(2)}, u32[]{:S(2)}) collective-permute-start(bf16[1,2,256,512]{3,2,1,0:T(8,128)(2,1)S(1)} %bitcast.129), channel_id=1, source_target_pairs={{0,15},{1,14},{2,13},{3,12},{4,11},{5,10},{6,9},{7,8},{16,31},{17,... | collective-permute-start | bytes 1572872 | tf_op jit(solution)/shard_map/while/body/eval_jaxpr/ppermute | solution.py:75
  577.8 25.1 %collective-permute-start.2 = (bf16[1,2,256,512]{3,2,1,0:T(8,128)(2,1)S(1)}, bf16[1,2,256,512]{3,2,1,0:T(8,128)(2,1)S(1)}, u32[]{:S(2)}, u32[]{:S(2)}) collective-permute-start(bf16[1,2,256,512]{3,2,1,0:T(8,128)(2,1)S(1)} %bitcast.129), channel_id=1, source_target_pairs={{0,15},{1,14},{2,13},{3,12},{4,11},{5,10},{6,9},{7,8},{16,31},{17,... | collective-permute-start | bytes 1572872 | tf_op jit(solution)/shard_map/while/body/eval_jaxpr/ppermute | solution.py:75
  626.7 25.4 %collective-permute-start.2 = (bf16[1,2,256,512]{3,2,1,0:T(8,128)(2,1)S(1)}, bf16[1,2,256,512]{3,2,1,0:T(8,128)(2,1)S(1)}, u32[]{:S(2)}, u32[]{:S(2)}) collective-permute-start(bf16[1,2,256,512]{3,2,1,0:T(8,128)(2,1)S(1)} %bitcast.129), channel_id=1, source_target_pairs={{0,15},{1,14},{2,13},{3,12},{4,11},{5,10},{6,9},{7,8},{16,31},{17,... | collective-permute-start | bytes 1572872 | tf_op jit(solution)/shard_map/while/body/eval_jaxpr/ppermute | solution.py:75
  675.9 25.1 %collective-permute-start.2 = (bf16[1,2,256,512]{3,2,1,0:T(8,128)(2,1)S(1)}, bf16[1,2,256,512]{3,2,1,0:T(8,128)(2,1)S(1)}, u32[]{:S(2)}, u32[]{:S(2)}) collective-permute-start(bf16[1,2,256,512]{3,2,1,0:T(8,128)(2,1)S(1)} %bitcast.129), channel_id=1, source_target_pairs={{0,15},{1,14},{2,13},{3,12},{4,11},{5,10},{6,9},{7,8},{16,31},{17,... | collective-permute-start | bytes 1572872 | tf_op jit(solution)/shard_map/while/body/eval_jaxpr/ppermute | solution.py:75
  724.8 25.4 %collective-permute-start.2 = (bf16[1,2,256,512]{3,2,1,0:T(8,128)(2,1)S(1)}, bf16[1,2,256,512]{3,2,1,0:T(8,128)(2,1)S(1)}, u32[]{:S(2)}, u32[]{:S(2)}) collective-permute-start(bf16[1,2,256,512]{3,2,1,0:T(8,128)(2,1)S(1)} %bitcast.129), channel_id=1, source_target_pairs={{0,15},{1,14},{2,13},{3,12},{4,11},{5,10},{6,9},{7,8},{16,31},{17,... | collective-permute-start | bytes 1572872 | tf_op jit(solution)/shard_map/while/body/eval_jaxpr/ppermute | solution.py:75
  773.9 25.1 %collective-permute-start.2 = (bf16[1,2,256,512]{3,2,1,0:T(8,128)(2,1)S(1)}, bf16[1,2,256,512]{3,2,1,0:T(8,128)(2,1)S(1)}, u32[]{:S(2)}, u32[]{:S(2)}) collective-permute-start(bf16[1,2,256,512]{3,2,1,0:T(8,128)(2,1)S(1)} %bitcast.129), channel_id=1, source_target_pairs={{0,15},{1,14},{2,13},{3,12},{4,11},{5,10},{6,9},{7,8},{16,31},{17,... | collective-permute-start | bytes 1572872 | tf_op jit(solution)/shard_map/while/body/eval_jaxpr/ppermute | solution.py:75
  822.8 25.4 %collective-permute-start.2 = (bf16[1,2,256,512]{3,2,1,0:T(8,128)(2,1)S(1)}, bf16[1,2,256,512]{3,2,1,0:T(8,128)(2,1)S(1)}, u32[]{:S(2)}, u32[]{:S(2)}) collective-permute-start(bf16[1,2,256,512]{3,2,1,0:T(8,128)(2,1)S(1)} %bitcast.129), channel_id=1, source_target_pairs={{0,15},{1,14},{2,13},{3,12},{4,11},{5,10},{6,9},{7,8},{16,31},{17,... | collective-permute-start | bytes 1572872 | tf_op jit(solution)/shard_map/while/body/eval_jaxpr/ppermute | solution.py:75
  872.0 25.1 %collective-permute-start.2 = (bf16[1,2,256,512]{3,2,1,0:T(8,128)(2,1)S(1)}, bf16[1,2,256,512]{3,2,1,0:T(8,128)(2,1)S(1)}, u32[]{:S(2)}, u32[]{:S(2)}) collective-permute-start(bf16[1,2,256,512]{3,2,1,0:T(8,128)(2,1)S(1)} %bitcast.129), channel_id=1, source_target_pairs={{0,15},{1,14},{2,13},{3,12},{4,11},{5,10},{6,9},{7,8},{16,31},{17,... | collective-permute-start | bytes 1572872 | tf_op jit(solution)/shard_map/while/body/eval_jaxpr/ppermute | solution.py:75
  920.9 25.4 %collective-permute-start.2 = (bf16[1,2,256,512]{3,2,1,0:T(8,128)(2,1)S(1)}, bf16[1,2,256,512]{3,2,1,0:T(8,128)(2,1)S(1)}, u32[]{:S(2)}, u32[]{:S(2)}) collective-permute-start(bf16[1,2,256,512]{3,2,1,0:T(8,128)(2,1)S(1)} %bitcast.129), channel_id=1, source_target_pairs={{0,15},{1,14},{2,13},{3,12},{4,11},{5,10},{6,9},{7,8},{16,31},{17,... | collective-permute-start | bytes 1572872 | tf_op jit(solution)/shard_map/while/body/eval_jaxpr/ppermute | solution.py:75
  970.1 25.1 %collective-permute-start.2 = (bf16[1,2,256,512]{3,2,1,0:T(8,128)(2,1)S(1)}, bf16[1,2,256,512]{3,2,1,0:T(8,128)(2,1)S(1)}, u32[]{:S(2)}, u32[]{:S(2)}) collective-permute-start(bf16[1,2,256,512]{3,2,1,0:T(8,128)(2,1)S(1)} %bitcast.129), channel_id=1, source_target_pairs={{0,15},{1,14},{2,13},{3,12},{4,11},{5,10},{6,9},{7,8},{16,31},{17,... | collective-permute-start | bytes 1572872 | tf_op jit(solution)/shard_map/while/body/eval_jaxpr/ppermute | solution.py:75
  1019.0 25.4 %collective-permute-start.2 = (bf16[1,2,256,512]{3,2,1,0:T(8,128)(2,1)S(1)}, bf16[1,2,256,512]{3,2,1,0:T(8,128)(2,1)S(1)}, u32[]{:S(2)}, u32[]{:S(2)}) collective-permute-start(bf16[1,2,256,512]{3,2,1,0:T(8,128)(2,1)S(1)} %bitcast.129), channel_id=1, source_target_pairs={{0,15},{1,14},{2,13},{3,12},{4,11},{5,10},{6,9},{7,8},{16,31},{17,... | collective-permute-start | bytes 1572872 | tf_op jit(solution)/shard_map/while/body/eval_jaxpr/ppermute | solution.py:75
  1068.1 25.1 %collective-permute-start.2 = (bf16[1,2,256,512]{3,2,1,0:T(8,128)(2,1)S(1)}, bf16[1,2,256,512]{3,2,1,0:T(8,128)(2,1)S(1)}, u32[]{:S(2)}, u32[]{:S(2)}) collective-permute-start(bf16[1,2,256,512]{3,2,1,0:T(8,128)(2,1)S(1)} %bitcast.129), channel_id=1, source_target_pairs={{0,15},{1,14},{2,13},{3,12},{4,11},{5,10},{6,9},{7,8},{16,31},{17,... | collective-permute-start | bytes 1572872 | tf_op jit(solution)/shard_map/while/body/eval_jaxpr/ppermute | solution.py:75
  1117.0 25.4 %collective-permute-start.2 = (bf16[1,2,256,512]{3,2,1,0:T(8,128)(2,1)S(1)}, bf16[1,2,256,512]{3,2,1,0:T(8,128)(2,1)S(1)}, u32[]{:S(2)}, u32[]{:S(2)}) collective-permute-start(bf16[1,2,256,512]{3,2,1,0:T(8,128)(2,1)S(1)} %bitcast.129), channel_id=1, source_target_pairs={{0,15},{1,14},{2,13},{3,12},{4,11},{5,10},{6,9},{7,8},{16,31},{17,... | collective-permute-start | bytes 1572872 | tf_op jit(solution)/shard_map/while/body/eval_jaxpr/ppermute | solution.py:75
  1166.2 25.1 %collective-permute-start.2 = (bf16[1,2,256,512]{3,2,1,0:T(8,128)(2,1)S(1)}, bf16[1,2,256,512]{3,2,1,0:T(8,128)(2,1)S(1)}, u32[]{:S(2)}, u32[]{:S(2)}) collective-permute-start(bf16[1,2,256,512]{3,2,1,0:T(8,128)(2,1)S(1)} %bitcast.129), channel_id=1, source_target_pairs={{0,15},{1,14},{2,13},{3,12},{4,11},{5,10},{6,9},{7,8},{16,31},{17,... | collective-permute-start | bytes 1572872 | tf_op jit(solution)/shard_map/while/body/eval_jaxpr/ppermute | solution.py:75
  1215.1 25.4 %collective-permute-start.2 = (bf16[1,2,256,512]{3,2,1,0:T(8,128)(2,1)S(1)}, bf16[1,2,256,512]{3,2,1,0:T(8,128)(2,1)S(1)}, u32[]{:S(2)}, u32[]{:S(2)}) collective-permute-start(bf16[1,2,256,512]{3,2,1,0:T(8,128)(2,1)S(1)} %bitcast.129), channel_id=1, source_target_pairs={{0,15},{1,14},{2,13},{3,12},{4,11},{5,10},{6,9},{7,8},{16,31},{17,... | collective-permute-start | bytes 1572872 | tf_op jit(solution)/shard_map/while/body/eval_jaxpr/ppermute | solution.py:75
  1264.3 25.1 %collective-permute-start.2 = (bf16[1,2,256,512]{3,2,1,0:T(8,128)(2,1)S(1)}, bf16[1,2,256,512]{3,2,1,0:T(8,128)(2,1)S(1)}, u32[]{:S(2)}, u32[]{:S(2)}) collective-permute-start(bf16[1,2,256,512]{3,2,1,0:T(8,128)(2,1)S(1)} %bitcast.129), channel_id=1, source_target_pairs={{0,15},{1,14},{2,13},{3,12},{4,11},{5,10},{6,9},{7,8},{16,31},{17,... | collective-permute-start | bytes 1572872 | tf_op jit(solution)/shard_map/while/body/eval_jaxpr/ppermute | solution.py:75
  1313.2 25.4 %collective-permute-start.2 = (bf16[1,2,256,512]{3,2,1,0:T(8,128)(2,1)S(1)}, bf16[1,2,256,512]{3,2,1,0:T(8,128)(2,1)S(1)}, u32[]{:S(2)}, u32[]{:S(2)}) collective-permute-start(bf16[1,2,256,512]{3,2,1,0:T(8,128)(2,1)S(1)} %bitcast.129), channel_id=1, source_target_pairs={{0,15},{1,14},{2,13},{3,12},{4,11},{5,10},{6,9},{7,8},{16,31},{17,... | collective-permute-start | bytes 1572872 | tf_op jit(solution)/shard_map/while/body/eval_jaxpr/ppermute | solution.py:75
  1362.3 25.1 %collective-permute-start.2 = (bf16[1,2,256,512]{3,2,1,0:T(8,128)(2,1)S(1)}, bf16[1,2,256,512]{3,2,1,0:T(8,128)(2,1)S(1)}, u32[]{:S(2)}, u32[]{:S(2)}) collective-permute-start(bf16[1,2,256,512]{3,2,1,0:T(8,128)(2,1)S(1)} %bitcast.129), channel_id=1, source_target_pairs={{0,15},{1,14},{2,13},{3,12},{4,11},{5,10},{6,9},{7,8},{16,31},{17,... | collective-permute-start | bytes 1572872 | tf_op jit(solution)/shard_map/while/body/eval_jaxpr/ppermute | solution.py:75
  1411.2 25.4 %collective-permute-start.2 = (bf16[1,2,256,512]{3,2,1,0:T(8,128)(2,1)S(1)}, bf16[1,2,256,512]{3,2,1,0:T(8,128)(2,1)S(1)}, u32[]{:S(2)}, u32[]{:S(2)}) collective-permute-start(bf16[1,2,256,512]{3,2,1,0:T(8,128)(2,1)S(1)} %bitcast.129), channel_id=1, source_target_pairs={{0,15},{1,14},{2,13},{3,12},{4,11},{5,10},{6,9},{7,8},{16,31},{17,... | collective-permute-start | bytes 1572872 | tf_op jit(solution)/shard_map/while/body/eval_jaxpr/ppermute | solution.py:75
  1460.4 25.1 %collective-permute-start.2 = (bf16[1,2,256,512]{3,2,1,0:T(8,128)(2,1)S(1)}, bf16[1,2,256,512]{3,2,1,0:T(8,128)(2,1)S(1)}, u32[]{:S(2)}, u32[]{:S(2)}) collective-permute-start(bf16[1,2,256,512]{3,2,1,0:T(8,128)(2,1)S(1)} %bitcast.129), channel_id=1, source_target_pairs={{0,15},{1,14},{2,13},{3,12},{4,11},{5,10},{6,9},{7,8},{16,31},{17,... | collective-permute-start | bytes 1572872 | tf_op jit(solution)/shard_map/while/body/eval_jaxpr/ppermute | solution.py:75
  1509.3 25.4 %collective-permute-start.2 = (bf16[1,2,256,512]{3,2,1,0:T(8,128)(2,1)S(1)}, bf16[1,2,256,512]{3,2,1,0:T(8,128)(2,1)S(1)}, u32[]{:S(2)}, u32[]{:S(2)}) collective-permute-start(bf16[1,2,256,512]{3,2,1,0:T(8,128)(2,1)S(1)} %bitcast.129), channel_id=1, source_target_pairs={{0,15},{1,14},{2,13},{3,12},{4,11},{5,10},{6,9},{7,8},{16,31},{17,... | collective-permute-start | bytes 1572872 | tf_op jit(solution)/shard_map/while/body/eval_jaxpr/ppermute | solution.py:75
  1558.5 25.1 %collective-permute-start.2 = (bf16[1,2,256,512]{3,2,1,0:T(8,128)(2,1)S(1)}, bf16[1,2,256,512]{3,2,1,0:T(8,128)(2,1)S(1)}, u32[]{:S(2)}, u32[]{:S(2)}) collective-permute-start(bf16[1,2,256,512]{3,2,1,0:T(8,128)(2,1)S(1)} %bitcast.129), channel_id=1, source_target_pairs={{0,15},{1,14},{2,13},{3,12},{4,11},{5,10},{6,9},{7,8},{16,31},{17,... | collective-permute-start | bytes 1572872 | tf_op jit(solution)/shard_map/while/body/eval_jaxpr/ppermute | solution.py:75
  (69 other events, 499.9 us)
where the time goes:
time: 1640 us; the launch traced here: 1630 us
  matrix products  507 us (31%)
  waiting for transfers between devices  426 us (26%)
  starting transfers between devices  365 us (22%)
  other arithmetic  182 us (11%)
  local copies, waits for them, and re-layouts  99.4 us (6%)
  blocking collectives  45 us (3%)
    ppermute x32, waiting for transfers between devices, step_body(): next_skips = lax.ppermute(jnp.stack(block_outs), 'stage', mirror_perm)  426 us
    ppermute x32, starting transfers between devices, step_body(): next_skips = lax.ppermute(jnp.stack(block_outs), 'stage', mirror_perm)  278 us
    dot_general x32, matrix products, value_a9(): jnp.einsum('btf,fd->btd', gelu_act, wdown_one, preferred_element_type=jnp...  176 us
    dot_general x32, matrix products, value_a9(): jnp.einsum('bqhd,hde->bqe', attended, wo_one, preferred_element_type=jnp....  134 us
    dot_general x32, matrix products, value_a9(): jnp.einsum('btd,de->bte', normed.astype(jnp.bfloat16), wqkv_one, preferre...  115 us
    sub x32, other arithmetic, value_a9(): attn_probs = jax.nn.softmax(scores, axis=-1).astype(jnp.bfloat16)  95.3 us
    ppermute x32, starting transfers between devices, step_body(): next_bound = lax.ppermute(stage_out, 'stage', chain_perm)  65.6 us
    reduce_sum x64, other arithmetic, layer_norm(): variance = jnp.mean(centered * centered, axis=-1, keepdims=True)  55.7 us
  transfers between devices with their start and end apart: 96, of which 32 were waited for; matrix products, arithmetic and copies ran while one was open for 5% of the time, Pallas kernels for 0%

commit v1 on v0

v1 whole, which is shorter than its diff:
```python
import functools
import math

import jax
import jax.numpy as jnp
from jax import lax
from jax.experimental import pallas as pl
from jax.experimental.pallas import tpu as pltpu
from jax.sharding import PartitionSpec as P

F32 = jnp.float32
BF16 = jnp.bfloat16
PIECE = 64
CHUNK = 256
NP = CHUNK // PIECE
CORES = 2
SLOTS = 4
EPS = 1e-6
LAG = 4
TANH_A = math.sqrt(2.0 / math.pi)
TANH_B = TANH_A * 0.044715


class Unit:
    def __init__(self):
        self.accs, self.next, self.rhs = {}, 0, None

    def alloc(self, count):
        ids = list(range(self.next, self.next + count))
        self.next += count
        return ids

    def push(self, rhs):
        self.rhs = rhs
        return 0

    def feed(self, reg, ids, lhs):
        for n, a in enumerate(ids):
            v = jnp.dot(lhs(n), self.rhs, preferred_element_type=F32)
            self.accs[a] = self.accs[a] + v if a in self.accs else v

    def pop(self, a):
        return self.accs.pop(a)


def accumulators():
    return []


def make_units(accs):
    return [Unit(), Unit()]


def norm_mod(h, scale, shift):
    width = h.shape[0]
    mean = jnp.sum(h, axis=0, keepdims=True) * (1.0 / width)
    c = h - mean
    var = jnp.sum(c * c, axis=0, keepdims=True) * (1.0 / width)
    return ((c * lax.rsqrt(var + EPS)) * scale + shift).astype(BF16)


def gelu(x):
    return (x * (0.5 + 0.5 * jnp.tanh(x * (TANH_A + TANH_B * (x * x))))).astype(BF16)


def softmax(s, scale):
    m = jnp.max(s, axis=0, keepdims=True)
    p = jnp.exp2((s - m) * (scale * math.log2(math.e)))
    return (p * (1.0 / jnp.sum(p, axis=0, keepdims=True))).astype(BF16)


def wide(cols):
    return jnp.concatenate([cols, cols], axis=1)


def spread(mods, dst):
    cols = mods.T
    for v in range(6):
        col = cols[:, v : v + 1]
        if v in (1, 4):
            col = 1.0 + col
        dst[v] = jnp.broadcast_to(col, dst.shape[1:])


def block(units, h_ref, mod, w_qkv, w_o, w_up, w_down, out, t, heads, extra):
    width, tokens = h_ref.shape
    ff = w_up.shape[0]
    dim = width // heads
    ktiles = width // CHUNK
    per_group = CHUNK // dim
    groups = heads // per_group

    def project(q, w, row, rhs, nk, done):
        u = units[q]
        ids = u.alloc(NP)
        for k in range(nk):
            reg = u.push(rhs(k))
            u.feed(reg, ids, lambda n: w[row + PIECE * n : row + PIECE * (n + 1), CHUNK * k : CHUNK * (k + 1)])
        for n, a in enumerate(ids):
            done(row + PIECE * n, u.pop(a))

    def u_tile(k):
        return t.u[CHUNK * k : CHUNK * (k + 1), :]

    t.u[...] = norm_mod(h_ref[...], wide(mod[1]), wide(mod[0]))

    def keep_qkv(row, v):
        t.qkv[row : row + PIECE, :] = v.astype(BF16)

    for part in (1, 0, 2):
        for g in range(groups):
            project(g % 2, w_qkv, width * part + CHUNK * g, u_tile, ktiles, keep_qkv)

    zero = jnp.zeros((dim, tokens), BF16)
    keys = [t.qkv[width + CHUNK * g : width + CHUNK * (g + 1), :].T for g in range(groups)]

    def scores(hd):
        g, j = divmod(hd, per_group)
        query = t.qkv[dim * hd : dim * (hd + 1), :]
        padded = jnp.concatenate([query if n == j else zero for n in range(per_group)], axis=0)
        u = units[g % 2]
        ids = u.alloc(NP)
        reg = u.push(padded)
        u.feed(reg, ids, lambda n: keys[g][PIECE * n : PIECE * (n + 1)])
        for n, a in enumerate(ids):
            t.s[g, j % 2, PIECE * n : PIECE * (n + 1), :] = u.pop(a)

    def probs(hd):
        g, j = divmod(hd, per_group)
        for c in range(0, tokens, 128):
            t.p[g, j % 2, :, c : c + 128] = softmax(t.s[g, j % 2, :, c : c + 128], 1.0 / math.sqrt(dim))

    def values(hd):
        g, j = divmod(hd, per_group)
        u = units[g % 2]
        reg = u.push(t.p[g, j % 2])
        ids = u.alloc(1)
        u.feed(reg, ids, lambda n: t.qkv[2 * width + dim * hd : 2 * width + dim * (hd + 1), :])
        t.o[dim * hd : dim * (hd + 1), :] = u.pop(ids[0]).astype(BF16)

    for g in range(groups):
        scores(g * per_group)
    for j in range(per_group):
        for g in range(groups):
            hd = g * per_group + j
            if j + 1 < per_group:
                scores(hd + 1)
            probs(hd)
            values(hd)

    def o_tile(k):
        return t.o[CHUNK * k : CHUNK * (k + 1), :]

    def add_attn(row, v):
        h_ref[row : row + PIECE, :] = h_ref[row : row + PIECE, :] + wide(mod[2, row : row + PIECE]) * v

    for n in range(width // CHUNK):
        project(n % 2, w_o, CHUNK * n, o_tile, ktiles, add_attn)

    t.u[...] = norm_mod(h_ref[...], wide(mod[4]), wide(mod[3]))
    down_ids = [u.alloc(NP) for u in units]
    chunks = ff // CHUNK

    def up(n):
        u = units[n % 2]
        ids = u.alloc(NP)
        for k in range(ktiles):
            reg = u.push(u_tile(k))
            u.feed(
                reg,
                ids,
                lambda m: w_up[CHUNK * n + PIECE * m : CHUNK * n + PIECE * (m + 1), CHUNK * k : CHUNK * (k + 1)],
            )
        return ids

    def down(k):
        for q, u in enumerate(units):
            reg = u.push(t.act[CHUNK * k : CHUNK * (k + 1), :])
            u.feed(
                reg,
                down_ids[q],
                lambda m: w_down[CHUNK * q + PIECE * m : CHUNK * q + PIECE * (m + 1), CHUNK * k : CHUNK * (k + 1)],
            )

    for n in range(chunks):
        ids = up(n)
        if n >= LAG:
            down(n - LAG)
        for m, a in enumerate(ids):
            t.act[CHUNK * n + PIECE * m : CHUNK * n + PIECE * (m + 1), :] = gelu(units[n % 2].pop(a))
        if n == 0:
            extra()
    for n in range(chunks - LAG, chunks):
        down(n)
    for q, u in enumerate(units):
        for m, a in enumerate(down_ids[q]):
            row = CHUNK * q + PIECE * m
            h = h_ref[row : row + PIECE, :] + wide(mod[5, row : row + PIECE]) * u.pop(a)
            out[row : row + PIECE, :] = h.astype(BF16)


class Scratch:
    pass


def solution(mesh):
    stages = mesh.shape["stage"]
    chips = stages // CORES

    def kernel(
        steps, heads,
        x_ref, hwarm_ref, swarm_ref, win_ref, wout_ref, wqkv_ref, wo_ref, wup_ref, wdown_ref, wskip_ref, mods_ref,
        keep_ref, noise_ref,
        out_ref,
        raw_qkv, raw_o, raw_up, raw_down, stg_qkv, stg_o, stg_up, stg_down, stg_mod,
        w_qkv, w_o, w_up, w_down, w_mod, raw_skip, w_skip, raw_warm, w_in, w_out,
        in_a, in_b, out_a, out_b, x_t, x_all, h_ref, s_u, s_qkv, s_o, s_act, s_s, s_p, mod_a, mod_b,
        load_sem, warm_sem, wsend_sem, wrecv_sem, fsend_sem, frecv_sem,
        asend_sem, arecv_sem, bsend_sem, brecv_sem, xsend_sem, xrecv_sem,
    ):
        me = lax.axis_index("stage")
        chip, core = me // CORES, lax.rem(me, CORES)
        pair = lax.rem(chips - chip, chips)
        sample = lax.rem(core + pair, CORES)
        last_pair = chips - 1

        def device(chip_, core_):
            return {"stage": chip_ * CORES + core_}

        raws = [raw_qkv, raw_o, raw_up, raw_down]
        homes = [wqkv_ref, wo_ref, wup_ref, wdown_ref]
        loads = [pltpu.make_async_copy(src.at[0], dst, load_sem.at[n]) for n, (src, dst) in enumerate(zip(homes, raws))]
        loads.append(pltpu.make_async_copy(mods_ref.at[:, 0], stg_mod, load_sem.at[4]))
        loads.append(pltpu.make_async_copy(wskip_ref.at[last_pair - pair], raw_skip, load_sem.at[5]))
        warm = [
            pltpu.make_async_copy(hwarm_ref.at[jnp.maximum(pair - 1, 0), sample], raw_warm.at[0], warm_sem.at[0]),
            pltpu.make_async_copy(hwarm_ref.at[stages - 2 - pair, sample], raw_warm.at[1], warm_sem.at[1]),
            pltpu.make_async_copy(swarm_ref.at[pair, sample], raw_warm.at[2], warm_sem.at[2]),
        ]
        for copy in loads + warm:
            copy.start()

        home_pair = jnp.minimum(me, stages - 1 - me)
        home_slot = jnp.where(me < chips, 0, 1)
        goal = lax.rem(chips - home_pair, chips)

        def turn(src, dst):
            cols = src.shape[1]

            def body(n, _):
                at = pl.multiple_of(n * CHUNK, CHUNK)
                dst[pl.ds(at, CHUNK), :] = src[:, pl.ds(at, CHUNK)].T
                return 0

            lax.fori_loop(0, cols // CHUNK, body, 0)

        stages_of = [stg_qkv, stg_o, stg_up, stg_down, stg_mod]
        slots_of = [w_qkv, w_o, w_up, w_down, w_mod]

        def part(n, slot, cc):
            half = slots_of[n].shape[1] // CORES
            return slots_of[n].at[slot, pl.ds(pl.multiple_of(cc * half, half), half)]

        def home_part(n, cc):
            half = stages_of[n].shape[0] // CORES
            return stages_of[n].at[pl.ds(cc * half, half)]

        def direct(n, cc):
            return pltpu.make_async_remote_copy(
                src_ref=home_part(n, cc),
                dst_ref=part(n, home_slot, cc),
                send_sem=wsend_sem.at[n, cc],
                recv_sem=wrecv_sem.at[home_slot, n],
                device_id=device(goal, cc),
                device_id_type=pl.DeviceIdType.MESH,
            )

        def stay(n, cc):
            return pltpu.make_async_copy(home_part(n, cc), part(n, home_slot, cc), wrecv_sem.at[home_slot, n])

        def forward(n, slot):
            return pltpu.make_async_remote_copy(
                src_ref=part(n, slot, core),
                dst_ref=part(n, slot, core),
                send_sem=fsend_sem.at[slot, n],
                recv_sem=frecv_sem.at[slot, n],
                device_id=device(chip, 1 - core),
                device_id_type=pl.DeviceIdType.MESH,
            )

        for n in range(5):
            loads[n].wait()
            if n < 4:
                turn(raws[n], stages_of[n])
            for cc in range(CORES):
                mine = goal * CORES + cc == me

                @pl.when(mine)
                def _():
                    stay(n, cc).start()

                @pl.when(jnp.logical_not(mine))
                def _():
                    direct(n, cc).start()

        loads[5].wait()
        turn(raw_skip.at[0 : raw_skip.shape[1]], w_skip.at[0])
        turn(raw_skip.at[raw_skip.shape[1] :], w_skip.at[1])
        for copy in warm:
            copy.wait()
        in_a[0] = raw_warm[0].T
        in_b[0] = raw_warm[1].T
        out_a[1] = raw_warm[2].T
        x_t[...] = x_ref[sample].T
        w_in[...] = jnp.zeros_like(w_in)
        w_in[:, 0 : win_ref.shape[0]] = win_ref[...].T
        w_out[...] = wout_ref[...].T

        for slot in range(2):
            for n in range(5):
                pltpu.make_async_copy(part(n, slot, core), part(n, slot, core), wrecv_sem.at[slot, n]).wait()
                forward(n, slot).start()
        for slot in range(2):
            for n in range(5):
                forward(n, slot).wait_recv()

        t = Scratch()
        t.u, t.qkv, t.o, t.act, t.s, t.p = s_u, s_qkv, s_o, s_act, s_s, s_p
        channels = x_ref.shape[2]

        def a_copy(k):
            return pltpu.make_async_remote_copy(
                src_ref=out_a.at[lax.rem(k, 2)],
                dst_ref=in_a.at[lax.rem(k + 1, SLOTS)],
                send_sem=asend_sem.at[lax.rem(k, 2)],
                recv_sem=arecv_sem.at[lax.rem(k + 1, SLOTS)],
                device_id=device(lax.rem(chip + chips - 1, chips), 1 - core),
                device_id_type=pl.DeviceIdType.MESH,
            )

        def a_stay(k):
            return pltpu.make_async_copy(
                out_a.at[lax.rem(k, 2)], in_b.at[lax.rem(k + 1, SLOTS)], brecv_sem.at[lax.rem(k + 1, SLOTS)]
            )

        def b_copy(k):
            return pltpu.make_async_remote_copy(
                src_ref=out_b.at[lax.rem(k, 2)],
                dst_ref=in_b.at[lax.rem(k + 1, SLOTS)],
                send_sem=bsend_sem.at[lax.rem(k, 2)],
                recv_sem=brecv_sem.at[lax.rem(k + 1, SLOTS)],
                device_id=device(lax.rem(chip + 1, chips), 1 - core),
                device_id_type=pl.DeviceIdType.MESH,
            )

        def landed(buf, sem, k):
            slot = lax.rem(k, SLOTS)
            pltpu.make_async_copy(buf.at[slot], buf.at[slot], sem.at[slot]).wait()

        def compute(*accs):
            units = make_units(accs)

            spread(w_mod[0, 0], mod_a)

            def step(k, _):
                slot = lax.rem(k, SLOTS)
                here, before = lax.rem(k, 2), lax.rem(k + 1, 2)

                @pl.when(k < steps - 1 - pair)
                def _():
                    @pl.when(pair == 0)
                    def _():
                        x_pad = jnp.concatenate(
                            [x_t[...].astype(BF16), jnp.zeros((CHUNK - channels, x_t.shape[1]), BF16)], axis=0
                        )
                        for q, u in enumerate(units):
                            ids = u.alloc(NP)
                            reg = u.push(x_pad)
                            u.feed(reg, ids, lambda n: w_in[CHUNK * q + PIECE * n : CHUNK * q + PIECE * (n + 1), :])
                            for n, a in enumerate(ids):
                                h_ref[CHUNK * q + PIECE * n : CHUNK * q + PIECE * (n + 1), :] = u.pop(a)

                    @pl.when(pair > 0)
                    def _():
                        @pl.when(k > 0)
                        def _():
                            landed(in_a, arecv_sem, k)

                        h_ref[...] = in_a[slot].astype(F32)

                    @pl.when(jnp.logical_and(k > 1, pair < last_pair))
                    def _():
                        a_copy(k - 2).wait_send()

                    block(
                        units, h_ref, mod_a, w_qkv.at[0], w_o.at[0], w_up.at[0], w_down.at[0], out_a.at[here], t, heads,
                        lambda: spread(w_mod[1, k], mod_b),
                    )

                    @pl.when(pair == last_pair)
                    def _():
                        a_stay(k).start()

                    @pl.when(jnp.logical_and(pair < last_pair, k < steps - 3 - pair))
                    def _():
                        a_copy(k).start()

                @pl.when(k == steps - 1 - pair)
                def _():
                    spread(w_mod[1, k], mod_b)

                @pl.when(k > 0)
                def _():
                    landed(in_b, brecv_sem, k)

                @pl.when(jnp.logical_and(k > 1, pair > 0))
                def _():
                    b_copy(k - 2).wait_send()

                for q, u in enumerate(units):
                    ids = u.alloc(NP)
                    for half in range(2):
                        for n in range(h_ref.shape[0] // CHUNK):
                            rows = slice(CHUNK * n, CHUNK * (n + 1))
                            reg = u.push(in_b[slot, rows, :] if half == 0 else out_a[before, rows, :])
                            u.feed(
                                reg,
                                ids,
                                lambda m: w_skip[half, CHUNK * q + PIECE * m : CHUNK * q + PIECE * (m + 1), rows],
                            )
                    for m, a in enumerate(ids):
                        h_ref[CHUNK * q + PIECE * m : CHUNK * q + PIECE * (m + 1), :] = u.pop(a)
                block(
                    units, h_ref, mod_b, w_qkv.at[1], w_o.at[1], w_up.at[1], w_down.at[1], out_b.at[here], t, heads,
                    lambda: spread(w_mod[0, jnp.minimum(k + 1, steps - 1)], mod_a),
                )

                @pl.when(pair > 0)
                def _():
                    b_copy(k).start()

                @pl.when(pair == 0)
                def _():
                    u = units[0]
                    [a] = u.alloc(1)
                    pad = jnp.zeros((PIECE - channels, CHUNK), BF16)
                    for n in range(h_ref.shape[0] // CHUNK):
                        rows = slice(CHUNK * n, CHUNK * (n + 1))
                        reg = u.push(out_b[here, rows, :])
                        u.feed(reg, [a], lambda _: jnp.concatenate([w_out[:, rows], pad], axis=0))
                    noise = u.pop(a)[0:channels, :]
                    x_t[...] = keep_ref[k] * x_t[...] + noise_ref[k] * noise

                return 0

            lax.fori_loop(0, steps - pair, step, 0)

        compute()

        count = steps - pair

        @pl.when(pair > 0)
        def _():
            b_copy(count - 2).wait_send()
            b_copy(count - 1).wait_send()

        for n in range(5):
            for cc in range(CORES):

                @pl.when(goal * CORES + cc != me)
                def _():
                    direct(n, cc).wait_send()

            for slot in range(2):
                forward(n, slot).wait_send()

        def share(n, who):
            return pltpu.make_async_remote_copy(
                src_ref=x_t,
                dst_ref=x_all.at[who],
                send_sem=xsend_sem.at[n],
                recv_sem=xrecv_sem.at[who],
                device_id={"stage": n},
                device_id_type=pl.DeviceIdType.MESH,
            )

        @pl.when(pair == 0)
        def _():
            for n in range(stages):

                @pl.when(n != me)
                def _():
                    share(n, sample).start()

            own = pltpu.make_async_copy(x_t, x_all.at[sample], xrecv_sem.at[sample])
            own.start()
            for n in range(stages):

                @pl.when(n != me)
                def _():
                    share(n, sample).wait_send()

        for n in range(CORES):
            pltpu.make_async_copy(x_t, x_all.at[n], xrecv_sem.at[n]).wait()
            out_ref[n] = x_all[n].T

    def local_run(x_init, h_warm, skip_warm, w_in, w_out, w_qkv, w_o, w_up, w_down, w_skip, ada_mods, keep, noise):
        batch, tokens, channels = x_init.shape
        width, ff = w_up.shape[1], w_up.shape[2]
        heads = w_o.shape[1]
        steps = ada_mods.shape[0]
        any_ = pl.BlockSpec(memory_space=pl.ANY)
        vmem = pl.BlockSpec(memory_space=pltpu.VMEM)
        smem = pl.BlockSpec(memory_space=pltpu.SMEM)
        V = pltpu.VMEM
        D = pltpu.SemaphoreType.DMA
        scratch = [
            V((width, 3 * width), BF16), V((width, width), BF16), V((width, ff), BF16), V((ff, width), BF16),
            V((3 * width, width), BF16), V((width, width), BF16), V((ff, width), BF16), V((width, ff), BF16),
            V((steps, 6, width), F32),
            V((2, 3 * width, width), BF16), V((2, width, width), BF16), V((2, ff, width), BF16), V((2, width, ff), BF16),
            V((2, steps, 6, width), F32),
            V((2 * width, width), BF16), V((2, width, width), BF16), V((3, tokens, width), BF16),
            V((width, CHUNK), BF16), V((channels, width), BF16),
            V((SLOTS, width, tokens), BF16), V((SLOTS, width, tokens), BF16),
            V((2, width, tokens), BF16), V((2, width, tokens), BF16),
            V((channels, tokens), F32), V((CORES, channels, tokens), F32), V((width, tokens), F32),
            V((width, tokens), BF16), V((3 * width, tokens), BF16), V((width, tokens), BF16), V((ff, tokens), BF16),
            V((2, 2, tokens, tokens), F32), V((2, 2, tokens, tokens), BF16),
            V((6, width, 128), F32), V((6, width, 128), F32),
            D((6,)), D((3,)), D((5, CORES)), D((2, 5)), D((2, 5)), D((2, 5)),
            D((2,)), D((SLOTS,)), D((2,)), D((SLOTS,)), D((stages,)), D((CORES,)),
        ]
        call = pl.pallas_call(
            functools.partial(kernel, steps, heads),
            out_shape=jax.ShapeDtypeStruct((batch, tokens, channels), F32),
            in_specs=[vmem, any_, any_, vmem, vmem, any_, any_, any_, any_, any_, any_, smem, smem],
            out_specs=vmem,
            scratch_shapes=scratch,
            compiler_params=pltpu.CompilerParams(has_side_effects=True, vmem_limit_bytes=60 * 2**20),
            name="staged_sampler",
        )
        return call(
            x_init, h_warm, skip_warm, w_in, w_out, w_qkv, w_o.reshape(1, width, width), w_up, w_down, w_skip, ada_mods,
            keep, noise,
        )

    in_specs = (P('data'), P(None, 'data'), P(None, 'data'), P(), P(), P('stage'), P('stage'), P('stage'), P('stage'), P(), P(None, 'stage'), P(), P())
    return jax.shard_map(local_run, mesh=mesh, in_specs=in_specs, out_specs=P('data'), check_vma=False)
```

time: 1640 us -> 777 us (0.47)
  Pallas kernels: 0 us -> 770 us
  matrix products: 507 us -> 0 us
  waiting for transfers between devices: 426 us -> 0 us
  starting transfers between devices: 365 us -> 0 us
  other arithmetic: 182 us -> 0 us
  local copies, waits for them, and re-layouts: 99.4 us -> 6.58 us
  blocking collectives: 45 us -> 0 us
    pallas_call x0 -> x1, Pallas kernels: none -> 770 us  [local_run(): call(x_init, h_warm, skip_warm, w_in, w_out, w_qkv, w_o.reshape(1, width,...]
    dot_general x192 -> x0, matrix products: 507 us -> none  [the longest x32 176 us: value_a9(): jnp.einsum('btf,fd->btd', gelu_act, wdown_one, preferred_element_type=jnp...]
    ppermute x96 -> x0, waiting for transfers between devices: 426 us -> none  [the longest x32 426 us: step_body(): next_skips = lax.ppermute(jnp.stack(block_outs), 'stage', mirror_perm)]
    ppermute x96 -> x0, starting transfers between devices: 365 us -> none  [the longest x32 278 us: step_body(): next_skips = lax.ppermute(jnp.stack(block_outs), 'stage', mirror_perm)]
    sub x32 -> x0, other arithmetic: 95.3 us -> none  [value_a9(): attn_probs = jax.nn.softmax(scores, axis=-1).astype(jnp.bfloat16)]
    reduce_sum x96 -> x0, other arithmetic: 60.5 us -> none  [the longest x64 55.7 us: layer_norm(): variance = jnp.mean(centered * centered, axis=-1, keepdims=True)]
    convert_element_type x32 -> x0, local copies, waits for them, and re-layouts: 54.4 us -> none  [value_a9(): jnp.einsum('btd,de->bte', normed.astype(jnp.bfloat16), wqkv_one, preferre...]
    psum x1 -> x0, blocking collectives: 45 us -> none  [local_run(): lax.psum(jnp.where(stage_id == stages - 1, final_latent, jnp.zeros_like(f...]
  transfers between devices with their start and end apart: 96 -> 0, of which waited for: 32 -> 0; matrix products, arithmetic and copies ran while one was open for 5% -> 0% of each run, Pallas kernels for 0% -> 0%
where the time goes in v1:
time: 777 us; the launch traced here: 776 us
  Pallas kernels  770 us (99%)
    pallas_call x1, Pallas kernels, local_run(): call(x_init, h_warm, skip_warm, w_in, w_out, w_qkv, w_o.reshape(1, width,...  770 us

profile of v1, /device:TPU:21, one launch (start us, length us, event | category | flops | bytes accessed | tf_op | source)
XLA Modules:
  0.0 776.3 jit_solution(5387652404827283022)
XLA Ops:
  0.0 1.5 copy.15.wout_ref
  1.5 1.6 copy.14.x_ref
  3.1 1.9 copy.16.mods_ref
  4.9 769.7 %staged_sampler.1 = f32[2,256,16]{2,1,0:T(8,128)} custom-call(f32[2,256,16]{2,1,0:T(8,128)} %copy.14.x_ref, bf16[15,2,256,512]{3,2,1,0:T(8,128)(2,1)} %hwarm_ref.1, bf16[8,2,256,512]{3,2,1,0:T(8,128)(2,1)} %swarm_ref.1, bf16[16,512]{1,0:T(8,128)(2,1)} %win_ref.1, bf16[512,16]{1,0:T(8,128)(2,1)} %copy.15.wout_ref, bf16[1,512,1536]{2,1,0:T(8,128)(2,1)} %wqkv_ref.1, ...), custom_call_target="tpu_custom_call" | custom-call | tf_op jit(solution)/shard_map/staged_sampler/pallas_call | solution.py:543
  774.6 1.7 copy.17

commit v2 on v0

v2 whole, which is shorter than its diff:
```python
import functools
import math

import jax
import jax.numpy as jnp
from jax import lax
from jax.experimental import pallas as pl
from jax.experimental.pallas import tpu as pltpu
from jax.sharding import PartitionSpec as P

F32 = jnp.float32
BF16 = jnp.bfloat16
CHUNK = 256
CORES = 2
COLUMNS = 4
SHARES = CORES * COLUMNS
PIECES = 3
SLOTS = 4
EPS = 1e-6
TANH_A = math.sqrt(2.0 / math.pi)
TANH_B = TANH_A * 0.044715


def product(lhs, rhs):
    return jnp.dot(lhs, rhs, preferred_element_type=F32)


def norm_mod(h, scale, shift):
    width = h.shape[0]
    mean = jnp.sum(h, axis=0, keepdims=True) * (1.0 / width)
    c = h - mean
    var = jnp.sum(c * c, axis=0, keepdims=True) * (1.0 / width)
    return ((c * lax.rsqrt(var + EPS)) * scale + shift).astype(BF16)


def gelu(x):
    return (x * (0.5 + 0.5 * jnp.tanh(x * (TANH_A + TANH_B * (x * x))))).astype(BF16)


def softmax(s, scale):
    m = jnp.max(s, axis=0, keepdims=True)
    p = jnp.exp2((s - m) * (scale * math.log2(math.e)))
    return (p * (1.0 / jnp.sum(p, axis=0, keepdims=True))).astype(BF16)


def wide(cols):
    return jnp.concatenate([cols, cols], axis=1)


def spread(mods, dst):
    cols = mods.T
    for v in range(6):
        col = cols[:, v : v + 1]
        if v in (1, 4):
            col = 1.0 + col
        dst[v] = jnp.broadcast_to(col, dst.shape[1:])


def block(h_ref, mod, w, out, t, heads, extra):
    width, tokens = h_ref.shape
    dim = width // heads
    per_group = CHUNK // dim
    groups = heads // per_group
    row_o, row_up = 3 * width, 4 * width
    ff = (w.shape[0] - row_up) // 2
    row_down = row_up + ff

    u = norm_mod(h_ref[...], wide(mod[1]), wide(mod[0]))
    t.qkv[...] = product(w[0:row_o], u).astype(BF16)

    zero = jnp.zeros((dim, tokens), BF16)
    keys = [t.qkv[width + CHUNK * g : width + CHUNK * (g + 1), :].T for g in range(groups)]
    order = [g * per_group + j for j in range(per_group) for g in range(groups)]

    def scores(n):
        g, j = divmod(order[n], per_group)
        query = t.qkv[dim * order[n] : dim * (order[n] + 1), :]
        padded = jnp.concatenate([query if m == j else zero for m in range(per_group)], axis=0)
        t.s[n % 2] = product(keys[g], padded)

    def probs(n):
        for c in range(0, tokens, 128):
            t.p[n % 2, :, c : c + 128] = softmax(t.s[n % 2, :, c : c + 128], 1.0 / math.sqrt(dim))

    def values(n):
        row = dim * order[n]
        t.o[row : row + dim, :] = product(t.qkv[2 * width + row : 2 * width + row + dim, :], t.p[n % 2]).astype(BF16)

    scores(0)
    for n in range(heads):
        if n + 1 < heads:
            scores(n + 1)
        probs(n)
        values(n)

    h_ref[...] = h_ref[...] + wide(mod[2]) * product(w[row_o:row_up], t.o[...])
    u = norm_mod(h_ref[...], wide(mod[4]), wide(mod[3]))
    chunks = ff // width

    def up(n):
        return product(w[row_up + width * n : row_up + width * (n + 1)], u)

    held, total = up(0), None
    for n in range(chunks):
        ahead = up(n + 1) if n + 1 < chunks else None
        t.act[width * n : width * (n + 1), :] = gelu(held)
        held = ahead
        if n == 0:
            extra()
        part = product(w[row_down + width * n : row_down + width * (n + 1)], t.act[width * n : width * (n + 1), :])
        total = part if total is None else total + part
    out[...] = (h_ref[...] + wide(mod[5]) * total).astype(BF16)


class Scratch:
    pass


def solution(mesh):
    stages = mesh.shape["stage"]
    chips = stages // CORES
    side = math.isqrt(mesh.shape["data"])
    if side * side != mesh.shape["data"] or side % 2:
        raise ValueError("data axis")

    def kernel(
        steps, heads,
        x_ref, hwarm_ref, swarm_ref, win_ref, wout_ref, wqkv_ref, wo_ref, wup_ref, wdown_ref, wskip_ref, mods_ref,
        keep_ref, noise_ref,
        out_ref,
        raw_qkv, raw_o, raw_up, raw_down, home_w, home_mod, all_w, all_mod,
        raw_skip, w_skip, raw_warm, w_in, w_out,
        in_a, in_b, out_a, out_b, x_t, x_all, h_ref, s_qkv, s_o, s_act, s_s, s_p, mod_a, mod_b,
        load_sem, warm_sem, hsend_sem, get_sem, send_sem, put_sem, peer_sem,
        asend_sem, arecv_sem, bsend_sem, brecv_sem, xsend_sem, xrecv_sem,
    ):
        me = lax.axis_index("stage")
        group = lax.axis_index("data")
        chip, core = me // CORES, lax.rem(me, CORES)
        pair = lax.rem(chips - chip, chips)
        sample = lax.rem(core + pair, CORES)
        last_pair = chips - 1
        width = raw_o.shape[0]
        n_parts = PIECES + 1

        odd_x, odd_y = lax.rem(group // side, 2), lax.rem(group, 2)
        column = 2 * odd_x + odd_y
        next_x = {"data": group + side * (1 - 2 * odd_x), "stage": me}
        next_y = {"data": group + 1 - 2 * odd_y, "stage": me}
        peer = {"data": group, "stage": chip * CORES + 1 - core}
        beside_x, beside_y = 2 * (1 - odd_x) + odd_y, 2 * odd_x + 1 - odd_y
        across = 2 * (1 - odd_x) + 1 - odd_y

        def remote(src, dst, send, recv, to):
            return pltpu.make_async_remote_copy(
                src_ref=src, dst_ref=dst, send_sem=send, recv_sem=recv, device_id=to, device_id_type=pl.DeviceIdType.MESH
            )

        def arrived(ref, sem):
            pltpu.make_async_copy(ref, ref, sem).wait()

        raws = [raw_qkv, raw_o, raw_up, raw_down]
        homes = [wqkv_ref, wo_ref, wup_ref, wdown_ref]
        loads = [pltpu.make_async_copy(src.at[0], dst, load_sem.at[n]) for n, (src, dst) in enumerate(zip(homes, raws))]
        loads.append(pltpu.make_async_copy(mods_ref.at[:, 0], home_mod, load_sem.at[4]))
        loads.append(pltpu.make_async_copy(wskip_ref.at[last_pair - pair], raw_skip, load_sem.at[5]))
        warm = [
            pltpu.make_async_copy(hwarm_ref.at[jnp.maximum(pair - 1, 0), sample], raw_warm.at[0], warm_sem.at[0]),
            pltpu.make_async_copy(hwarm_ref.at[stages - 2 - pair, sample], raw_warm.at[1], warm_sem.at[1]),
            pltpu.make_async_copy(swarm_ref.at[pair, sample], raw_warm.at[2], warm_sem.at[2]),
        ]
        for n in (4, 0, 1, 2, 3, 5):
            loads[n].start()
        for copy in warm:
            copy.start()

        def turn(src, dst, row):
            def body(n, _):
                at = pl.multiple_of(n * CHUNK, CHUNK)
                dst[pl.ds(row + at, CHUNK), :] = src[:, pl.ds(at, CHUNK)].T
                return 0

            lax.fori_loop(0, src.shape[1] // CHUNK, body, 0)

        home_pair = jnp.minimum(me, stages - 1 - me)
        home_slot = jnp.where(me < chips, 0, 1)
        goal = lax.rem(chips - home_pair, chips)

        piece = home_w.shape[0] // PIECES
        share = piece // SHARES
        mod_share = steps // SHARES

        def whole(n, slot=None):
            if n == 0:
                return home_mod if slot is None else all_mod.at[slot]
            rows = pl.ds((n - 1) * piece, piece)
            return home_w.at[rows] if slot is None else all_w.at[slot, rows]

        def part(n, core_, column_, slot=None, half=None):
            at, size = core_ * COLUMNS + column_, mod_share if n == 0 else share
            at = at * size
            if half is not None:
                size //= 2
                at = at + half * size
            if n == 0:
                return home_mod.at[pl.ds(at, size)] if slot is None else all_mod.at[slot, pl.ds(at, size)]
            rows = pl.ds(pl.multiple_of((n - 1) * piece + at, 16), size)
            return home_w.at[rows] if slot is None else all_w.at[slot, rows]

        def leave(n, to_core):
            return remote(
                part(n, to_core, column), part(n, to_core, column, home_slot), hsend_sem.at[n, to_core],
                get_sem.at[home_slot, n], {"data": group, "stage": goal * CORES + to_core},
            )

        def stay(n):
            return pltpu.make_async_copy(whole(n), whole(n, home_slot), get_sem.at[home_slot, n])

        def hand(n):
            return remote(whole(n), whole(n, home_slot), hsend_sem.at[n, 0], get_sem.at[home_slot, n], peer)

        def send_home(n):
            @pl.when(goal == chip)
            def _():
                stay(n).start()
                hand(n).start()

            @pl.when(goal != chip)
            def _():
                for to_core in range(CORES):
                    leave(n, to_core).start()

        loads[4].wait()
        send_home(0)
        loads[0].wait()
        turn(raw_qkv, home_w, 0)
        loads[1].wait()
        turn(raw_o, home_w, 3 * width)
        send_home(1)
        loads[2].wait()
        turn(raw_up, home_w, 4 * width)
        send_home(2)
        loads[3].wait()
        for n in range(raw_down.shape[0] // width):
            turn(raw_down.at[width * n : width * (n + 1)], home_w, 4 * width + raw_up.shape[1] + width * n)
        send_home(3)

        loads[5].wait()
        turn(raw_skip.at[0:width], w_skip.at[0], 0)
        turn(raw_skip.at[width : 2 * width], w_skip.at[1], 0)
        for copy in warm:
            copy.wait()
        in_a[0] = raw_warm[0].T
        in_b[0] = raw_warm[1].T
        out_a[1] = raw_warm[2].T
        x_t[...] = x_ref[sample].T
        w_in[...] = jnp.zeros_like(w_in)
        w_in[:, 0 : win_ref.shape[0]] = win_ref[...].T
        w_out[...] = wout_ref[...].T

        def gather(slot):
            def to_x(n):
                ref = part(n, core, column, slot)
                return remote(ref, ref, send_sem.at[slot, n, 0], put_sem.at[slot, n, 0], next_x)

            def to_y(n):
                ref = part(n, core, column, slot)
                return remote(ref, ref, send_sem.at[slot, n, 1], put_sem.at[slot, n, 1], next_y)

            def on_y(n):
                ref = part(n, core, beside_x, slot, 0)
                return remote(ref, ref, send_sem.at[slot, n, 2], put_sem.at[slot, n, 2], next_y)

            def on_x(n):
                ref = part(n, core, beside_y, slot, 1)
                return remote(ref, ref, send_sem.at[slot, n, 3], put_sem.at[slot, n, 3], next_x)

            def to_peer(n, m):
                ref = part(n, core, [column, beside_x, beside_y, across][m], slot)
                return remote(ref, ref, send_sem.at[slot, n, 4 + m], peer_sem.at[slot, n, m], peer)

            def first(n):
                arrived(part(n, core, column, slot), get_sem.at[slot, n])
                to_x(n).start()
                to_y(n).start()
                to_peer(n, 0).start()

            def second(n):
                arrived(part(n, core, beside_x, slot), put_sem.at[slot, n, 0])
                on_y(n).start()
                to_peer(n, 1).start()
                arrived(part(n, core, beside_y, slot), put_sem.at[slot, n, 1])
                on_x(n).start()
                to_peer(n, 2).start()

            def third(n):
                arrived(part(n, core, across, slot, 0), put_sem.at[slot, n, 2])
                arrived(part(n, core, across, slot, 1), put_sem.at[slot, n, 3])
                to_peer(n, 3).start()

            def last(n):
                for m, c in enumerate([column, beside_x, beside_y, across]):
                    arrived(part(n, 1 - core, c, slot), peer_sem.at[slot, n, m])

            def sent(n):
                for copy in (to_x(n), to_y(n), on_y(n), on_x(n), *(to_peer(n, m) for m in range(4))):
                    copy.wait_send()

            return first, second, third, last, sent

        local = [pair // CORES == chip, (stages - 1 - pair) // CORES == chip]
        for slot in range(2):
            first, second, third, last, _ = gather(slot)

            @pl.when(local[slot])
            def _():
                for n in range(n_parts):
                    arrived(whole(n, slot), get_sem.at[slot, n])

            @pl.when(jnp.logical_not(local[slot]))
            def _():
                for n in range(n_parts + 2):
                    if n < n_parts:
                        first(n)
                    if 1 <= n <= n_parts:
                        second(n - 1)
                    if n >= 2:
                        third(n - 2)
                for n in range(n_parts):
                    last(n)

        t = Scratch()
        t.qkv, t.o, t.act, t.s, t.p = s_qkv, s_o, s_act, s_s, s_p
        channels = x_ref.shape[2]

        def a_copy(k):
            return remote(
                out_a.at[lax.rem(k, 2)], in_a.at[lax.rem(k + 1, SLOTS)], asend_sem.at[lax.rem(k, 2)],
                arecv_sem.at[lax.rem(k + 1, SLOTS)],
                {"data": group, "stage": lax.rem(chip + chips - 1, chips) * CORES + 1 - core},
            )

        def a_stay(k):
            slot = lax.rem(k + 1, SLOTS)
            return pltpu.make_async_copy(out_a.at[lax.rem(k, 2)], in_b.at[slot], brecv_sem.at[slot])

        def b_copy(k):
            return remote(
                out_b.at[lax.rem(k, 2)], in_b.at[lax.rem(k + 1, SLOTS)], bsend_sem.at[lax.rem(k, 2)],
                brecv_sem.at[lax.rem(k + 1, SLOTS)],
                {"data": group, "stage": lax.rem(chip + 1, chips) * CORES + 1 - core},
            )

        spread(all_mod[0, 0], mod_a)

        def step(k, _):
            slot = lax.rem(k, SLOTS)
            here, before = lax.rem(k, 2), lax.rem(k + 1, 2)

            @pl.when(k < steps - 1 - pair)
            def _():
                @pl.when(pair == 0)
                def _():
                    fill = jnp.zeros((CHUNK - channels, x_t.shape[1]), BF16)
                    h_ref[...] = product(w_in[...], jnp.concatenate([x_t[...].astype(BF16), fill], axis=0))

                @pl.when(pair > 0)
                def _():
                    @pl.when(k > 0)
                    def _():
                        arrived(in_a.at[slot], arecv_sem.at[slot])

                    h_ref[...] = in_a[slot].astype(F32)

                @pl.when(jnp.logical_and(k > 1, pair < last_pair))
                def _():
                    a_copy(k - 2).wait_send()

                block(h_ref, mod_a, all_w.at[0], out_a.at[here], t, heads, lambda: spread(all_mod[1, k], mod_b))

                @pl.when(pair == last_pair)
                def _():
                    a_stay(k).start()

                @pl.when(jnp.logical_and(pair < last_pair, k < steps - 3 - pair))
                def _():
                    a_copy(k).start()

            @pl.when(k == steps - 1 - pair)
            def _():
                spread(all_mod[1, k], mod_b)

            @pl.when(k > 0)
            def _():
                arrived(in_b.at[slot], brecv_sem.at[slot])

            @pl.when(jnp.logical_and(k > 1, pair > 0))
            def _():
                b_copy(k - 2).wait_send()

            h_ref[...] = product(w_skip[1], out_a[before]) + product(w_skip[0], in_b[slot])
            block(
                h_ref, mod_b, all_w.at[1], out_b.at[here], t, heads,
                lambda: spread(all_mod[0, jnp.minimum(k + 1, steps - 1)], mod_a),
            )

            @pl.when(pair > 0)
            def _():
                b_copy(k).start()

            @pl.when(pair == 0)
            def _():
                x_t[...] = keep_ref[k] * x_t[...] + noise_ref[k] * product(w_out[...], out_b[here])

            return 0

        lax.fori_loop(0, steps - pair, step, 0)

        def tell(n):
            return remote(x_t, x_all.at[sample], xsend_sem.at[n], xrecv_sem.at[sample], {"data": group, "stage": n})

        @pl.when(pair == 0)
        def _():
            for n in range(stages):

                @pl.when(n != me)
                def _():
                    tell(n).start()

            pltpu.make_async_copy(x_t, x_all.at[sample], xrecv_sem.at[sample]).start()

        count = steps - pair

        @pl.when(pair > 0)
        def _():
            b_copy(count - 2).wait_send()
            b_copy(count - 1).wait_send()

        for n in range(n_parts):

            @pl.when(goal == chip)
            def _():
                hand(n).wait_send()

            @pl.when(goal != chip)
            def _():
                for to_core in range(CORES):
                    leave(n, to_core).wait_send()

        for slot in range(2):

            @pl.when(jnp.logical_not(local[slot]))
            def _():
                for n in range(n_parts):
                    gather(slot)[4](n)

        @pl.when(pair == 0)
        def _():
            for n in range(stages):

                @pl.when(n != me)
                def _():
                    tell(n).wait_send()

        for n in range(CORES):
            arrived(x_all.at[n], xrecv_sem.at[n])
            out_ref[n] = x_all[n].T

    def local_run(x_init, h_warm, skip_warm, w_in, w_out, w_qkv, w_o, w_up, w_down, w_skip, ada_mods, keep, noise):
        batch, tokens, channels = x_init.shape
        width, ff = w_up.shape[1], w_up.shape[2]
        heads = w_o.shape[1]
        steps = ada_mods.shape[0]
        rows = 4 * width + 2 * ff
        any_ = pl.BlockSpec(memory_space=pl.ANY)
        vmem = pl.BlockSpec(memory_space=pltpu.VMEM)
        smem = pl.BlockSpec(memory_space=pltpu.SMEM)
        V = pltpu.VMEM
        D = pltpu.SemaphoreType.DMA
        scratch = [
            V((width, 3 * width), BF16), V((width, width), BF16), V((width, ff), BF16), V((ff, width), BF16),
            V((rows, width), BF16), V((steps, 6, width), F32), V((2, rows, width), BF16), V((2, steps, 6, width), F32),
            V((2 * width, width), BF16), V((2, width, width), BF16), V((3, tokens, width), BF16),
            V((width, CHUNK), BF16), V((channels, width), BF16),
            V((SLOTS, width, tokens), BF16), V((SLOTS, width, tokens), BF16),
            V((2, width, tokens), BF16), V((2, width, tokens), BF16),
            V((channels, tokens), F32), V((CORES, channels, tokens), F32), V((width, tokens), F32),
            V((3 * width, tokens), BF16), V((width, tokens), BF16), V((ff, tokens), BF16),
            V((2, tokens, tokens), F32), V((2, tokens, tokens), BF16),
            V((6, width, 128), F32), V((6, width, 128), F32),
            D((6,)), D((3,)), D((PIECES + 1, CORES)), D((2, PIECES + 1)), D((2, PIECES + 1, 8)), D((2, PIECES + 1, 4)),
            D((2, PIECES + 1, 4)),
            D((2,)), D((SLOTS,)), D((2,)), D((SLOTS,)), D((stages,)), D((CORES,)),
        ]
        call = pl.pallas_call(
            functools.partial(kernel, steps, heads),
            out_shape=jax.ShapeDtypeStruct((batch, tokens, channels), F32),
            in_specs=[vmem, any_, any_, vmem, vmem, any_, any_, any_, any_, any_, any_, smem, smem],
            out_specs=vmem,
            scratch_shapes=scratch,
            compiler_params=pltpu.CompilerParams(has_side_effects=True, vmem_limit_bytes=60 * 2**20),
            name="staged_sampler",
        )
        return call(
            x_init, h_warm, skip_warm, w_in, w_out, w_qkv, w_o.reshape(1, width, width), w_up, w_down, w_skip, ada_mods,
            keep, noise,
        )

    in_specs = (P('data'), P(None, 'data'), P(None, 'data'), P(), P(), P('stage'), P('stage'), P('stage'), P('stage'), P(), P(None, 'stage'), P(), P())
    return jax.shard_map(local_run, mesh=mesh, in_specs=in_specs, out_specs=P('data'), check_vma=False)
```

time: 1640 us -> 531 us (0.32)
  Pallas kernels: 0 us -> 524 us
  matrix products: 507 us -> 0 us
  waiting for transfers between devices: 426 us -> 0 us
  starting transfers between devices: 365 us -> 0 us
  other arithmetic: 182 us -> 0 us
  local copies, waits for them, and re-layouts: 99.4 us -> 6.58 us
  blocking collectives: 45 us -> 0 us
    pallas_call x0 -> x1, Pallas kernels: none -> 524 us  [local_run(): call(x_init, h_warm, skip_warm, w_in, w_out, w_qkv, w_o.reshape(1, width,...]
    dot_general x192 -> x0, matrix products: 507 us -> none  [the longest x32 176 us: value_a9(): jnp.einsum('btf,fd->btd', gelu_act, wdown_one, preferred_element_type=jnp...]
    ppermute x96 -> x0, waiting for transfers between devices: 426 us -> none  [the longest x32 426 us: step_body(): next_skips = lax.ppermute(jnp.stack(block_outs), 'stage', mirror_perm)]
    ppermute x96 -> x0, starting transfers between devices: 365 us -> none  [the longest x32 278 us: step_body(): next_skips = lax.ppermute(jnp.stack(block_outs), 'stage', mirror_perm)]
    sub x32 -> x0, other arithmetic: 95.3 us -> none  [value_a9(): attn_probs = jax.nn.softmax(scores, axis=-1).astype(jnp.bfloat16)]
    reduce_sum x96 -> x0, other arithmetic: 60.5 us -> none  [the longest x64 55.7 us: layer_norm(): variance = jnp.mean(centered * centered, axis=-1, keepdims=True)]
    convert_element_type x32 -> x0, local copies, waits for them, and re-layouts: 54.4 us -> none  [value_a9(): jnp.einsum('btd,de->bte', normed.astype(jnp.bfloat16), wqkv_one, preferre...]
    psum x1 -> x0, blocking collectives: 45 us -> none  [local_run(): lax.psum(jnp.where(stage_id == stages - 1, final_latent, jnp.zeros_like(f...]
  transfers between devices with their start and end apart: 96 -> 0, of which waited for: 32 -> 0; matrix products, arithmetic and copies ran while one was open for 5% -> 0% of each run, Pallas kernels for 0% -> 0%
where the time goes in v2:
time: 531 us; the launch traced here: 530 us
  Pallas kernels  524 us (99%)
  local copies, waits for them, and re-layouts  6.58 us (1%)
    pallas_call x1, Pallas kernels, local_run(): call(x_init, h_warm, skip_warm, w_in, w_out, w_qkv, w_o.reshape(1, width,...  524 us

profile of v2, /device:TPU:21, one launch (start us, length us, event | category | flops | bytes accessed | tf_op | source)
XLA Modules:
  0.0 530.3 jit_solution(8067586113752311284)
XLA Ops:
  0.0 1.5 copy.15.wout_ref
  1.5 1.6 copy.14.x_ref
  3.1 1.9 copy.16.mods_ref
  4.9 523.7 %staged_sampler.1 = f32[2,256,16]{2,1,0:T(8,128)} custom-call(f32[2,256,16]{2,1,0:T(8,128)} %copy.14.x_ref, bf16[15,2,256,512]{3,2,1,0:T(8,128)(2,1)} %hwarm_ref.1, bf16[8,2,256,512]{3,2,1,0:T(8,128)(2,1)} %swarm_ref.1, bf16[16,512]{1,0:T(8,128)(2,1)} %win_ref.1, bf16[512,16]{1,0:T(8,128)(2,1)} %copy.15.wout_ref, bf16[1,512,1536]{2,1,0:T(8,128)(2,1)} %wqkv_ref.1, ...), custom_call_target="tpu_custom_call" | custom-call | tf_op jit(solution)/shard_map/staged_sampler/pallas_call | solution.py:504
  528.6 1.7 copy.17

commit v3 on v0

v3 whole, which is shorter than its diff:
```python
import functools
import math

import jax
import jax.numpy as jnp
from jax import lax
from jax.experimental import pallas as pl
from jax.experimental.pallas import tpu as pltpu
from jax.sharding import PartitionSpec as P

F32 = jnp.float32
BF16 = jnp.bfloat16
CHUNK = 256
CORES = 2
COLUMNS = 4
PIECES = 6
LATE_OWN = (8, 9)
LATE_PEER = 3
SLOTS = 4
EPS = 1e-6
AHEAD = 3
TANH_A = math.sqrt(2.0 / math.pi)
TANH_B = TANH_A * 0.044715


def product(lhs, rhs):
    return jnp.dot(lhs, rhs, preferred_element_type=F32)


def norm_mod(h, scale, shift):
    width = h.shape[0]
    mean = jnp.sum(h, axis=0, keepdims=True) * (1.0 / width)
    c = h - mean
    var = jnp.sum(c * c, axis=0, keepdims=True) * (1.0 / width)
    return ((c * lax.rsqrt(var + EPS)) * scale + shift).astype(BF16)


def gelu(x):
    return (x * (0.5 + 0.5 * jnp.tanh(x * (TANH_A + TANH_B * (x * x))))).astype(BF16)


def softmax(s, scale):
    m = jnp.max(s, axis=0, keepdims=True)
    p = jnp.exp2((s - m) * (scale * math.log2(math.e)))
    return (p * (1.0 / jnp.sum(p, axis=0, keepdims=True))).astype(BF16)


def wide(cols):
    return jnp.concatenate([cols, cols], axis=1)


def spread(mods, half, dst):
    rows = dst.shape[1] // 128
    cols = mods.T
    cols = jnp.where(half == 0, cols[:, 0 : 3 * rows], cols[:, 3 * rows : 6 * rows])
    for v in range(3):
        for n in range(rows):
            col = cols[:, rows * v + n : rows * v + n + 1]
            if v == 1:
                col = 1.0 + col
            dst[3 * half + v, 128 * n : 128 * (n + 1), :] = jnp.broadcast_to(col, (128, 128))


def block(h_ref, mod, w, out, t, heads, extra):
    width, tokens = h_ref.shape
    dim = width // heads
    per_group = CHUNK // dim
    groups = heads // per_group
    row_o, row_up = 3 * width, 4 * width
    ff = (w.shape[0] - row_up) // 2
    row_down = row_up + ff

    u = norm_mod(h_ref[...], wide(mod[1]), wide(mod[0]))
    for row in (width, 0, 2 * width):
        t.qkv[row : row + width] = product(w[row : row + width], u).astype(BF16)

    zero = jnp.zeros((dim, tokens), BF16)
    keys = [t.qkv[width + CHUNK * g : width + CHUNK * (g + 1), :].T for g in range(groups)]
    order = [g * per_group + j for j in range(per_group) for g in range(groups)]

    def scores(n):
        g, j = divmod(order[n], per_group)
        query = t.qkv[dim * order[n] : dim * (order[n] + 1), :]
        padded = jnp.concatenate([query if m == j else zero for m in range(per_group)], axis=0)
        t.s[n % (AHEAD + 1)] = product(keys[g], padded)

    def probs(n):
        for c in range(0, tokens, 128):
            t.p[n % 2, :, c : c + 128] = softmax(t.s[n % (AHEAD + 1), :, c : c + 128], 1.0 / math.sqrt(dim))

    def values(n):
        row = dim * order[n]
        t.o[row : row + dim, :] = product(t.qkv[2 * width + row : 2 * width + row + dim, :], t.p[n % 2]).astype(BF16)

    for n in range(AHEAD):
        scores(n)
    for n in range(heads):
        if n + AHEAD < heads:
            scores(n + AHEAD)
        probs(n)
        values(n)

    for row in range(0, width, CHUNK):
        rows = slice(row, row + CHUNK)
        h_ref[rows] = h_ref[rows] + wide(mod[2, rows]) * product(w[row_o + row : row_o + row + CHUNK], t.o[...])
    u = norm_mod(h_ref[...], wide(mod[4]), wide(mod[3]))
    chunks = ff // CHUNK

    def up(n):
        return product(w[row_up + CHUNK * n : row_up + CHUNK * (n + 1)], u)

    held, total = up(0), None
    for n in range(chunks):
        ahead = up(n + 1) if n + 1 < chunks else None
        rows = slice(CHUNK * n, CHUNK * (n + 1))
        t.act[rows, :] = gelu(held)
        held = ahead
        if n == 0:
            extra()
        at, col = divmod(CHUNK * n, width)
        part = product(w[row_down + width * at : row_down + width * (at + 1), col : col + CHUNK], t.act[rows, :])
        total = part if total is None else total + part
    out[...] = (h_ref[...] + wide(mod[5]) * total).astype(BF16)


class Scratch:
    pass


def solution(mesh):
    stages = mesh.shape["stage"]
    chips = stages // CORES
    side = math.isqrt(mesh.shape["data"])
    if side * side != mesh.shape["data"] or side % 2:
        raise ValueError("data axis")

    def kernel(
        steps, heads,
        x_ref, hwarm_ref, swarm_ref, win_ref, wout_ref, wqkv_ref, wo_ref, wup_ref, wdown_ref, wskip_ref, mods_ref,
        keep_ref, noise_ref,
        out_ref,
        raw_qkv, raw_o, raw_up, raw_down, home_w, home_mod, all_w, all_mod,
        raw_skip, w_skip, raw_warm, w_in,
        hub, outs, x_t, x_end, h_ref, s_qkv, s_o, s_act, s_s, s_p, mod_b,
        load_sem, warm_sem, hsend_sem, get_sem, send_sem, put_sem,
        csend_sem, crecv_sem, ssend_sem, srecv_sem, xsend_sem, xrecv_sem, esend_sem, erecv_sem,
        late_sem, ccredit_sem, scredit_sem,
    ):
        me = lax.axis_index("stage")
        group = lax.axis_index("data")
        chip, core = me // CORES, lax.rem(me, CORES)
        pair = lax.rem(chips - chip, chips)
        first_half, second_half = core == 0, core == 1
        stage = jnp.where(first_half, pair, stages - 1 - pair)
        last_pair = chips - 1
        samples, channels = x_ref.shape[0], x_ref.shape[1]
        width = raw_o.shape[0]
        n_parts = PIECES + 1
        mod_rows = 6 * width // 128
        mesh_ids = pl.DeviceIdType.MESH

        odd_x, odd_y = lax.rem(group // side, 2), lax.rem(group, 2)
        column = 2 * odd_x + odd_y
        next_x = {"data": group + side * (1 - 2 * odd_x), "stage": me}
        next_y = {"data": group + 1 - 2 * odd_y, "stage": me}
        beside_x, beside_y = 2 * (1 - odd_x) + odd_y, 2 * odd_x + 1 - odd_y
        across = 2 * (1 - odd_x) + 1 - odd_y

        def device(chip_, core_):
            return {"data": group, "stage": chip_ * CORES + core_}

        peer = device(chip, 1 - core)
        chain_to = device(jnp.where(first_half, lax.rem(chip + chips - 1, chips), lax.rem(chip + 1, chips)), core)
        chain_from = device(jnp.where(first_half, lax.rem(chip + 1, chips), lax.rem(chip + chips - 1, chips)), core)

        def remote(src, dst, send, recv, to):
            return pltpu.make_async_remote_copy(
                src_ref=src, dst_ref=dst, send_sem=send, recv_sem=recv, device_id=to, device_id_type=mesh_ids
            )

        def arrived(ref, sem):
            pltpu.make_async_copy(ref, ref, sem).wait()

        raws = [raw_qkv, raw_o, raw_up, raw_down]
        homes = [wqkv_ref, wo_ref, wup_ref, wdown_ref]
        loads = [pltpu.make_async_copy(src.at[0], dst, load_sem.at[n]) for n, (src, dst) in enumerate(zip(homes, raws))]
        loads.append(pltpu.make_async_copy(mods_ref, home_mod, load_sem.at[4]))
        loads.append(pltpu.make_async_copy(wskip_ref.at[last_pair - pair], raw_skip, load_sem.at[5]))
        chain_warm = jnp.maximum(stage - 1, 0)
        warm = [
            pltpu.make_async_copy(hwarm_ref.at[chain_warm], raw_warm.at[0], warm_sem.at[0]),
            pltpu.make_async_copy(swarm_ref.at[pair], raw_warm.at[1], warm_sem.at[1]),
        ]
        for n in (4, 0, 1, 2, 3, 5):
            loads[n].start()
        for copy in warm:
            copy.start()

        def turn(src, dst, row):
            for at in range(0, src.shape[1], CHUNK):
                dst[row + at : row + at + CHUNK, :] = src[:, at : at + CHUNK].T

        home_pair = jnp.minimum(me, stages - 1 - me)
        goal_chip, goal_core = lax.rem(chips - home_pair, chips), jnp.where(me < chips, 0, 1)
        goal = device(goal_chip, goal_core)
        here = jnp.logical_and(goal_chip == chip, goal_core == core)
        beside = jnp.logical_and(goal_chip == chip, goal_core != core)
        away = goal_chip != chip
        is_local = stage // CORES == chip
        piece = home_w.shape[0] // PIECES

        def part(n, ref_w, ref_mod, column_=None, half=None):
            size, at = (ref_mod.shape[0], 0) if n == 0 else (piece, (n - 1) * piece)
            if column_ is not None:
                size //= COLUMNS
                at = at + column_ * size
            if half is not None:
                size //= 2
                at = at + half * size
            rows = pl.ds(at if isinstance(at, int) else pl.multiple_of(at, 8 if n == 0 else 16), size)
            return (ref_mod if n == 0 else ref_w).at[rows]

        def home(n, column_=None):
            return part(n, home_w, home_mod, column_)

        def mine(n, column_=None, half=None):
            return part(n, all_w, all_mod, column_, half)

        def stay(n):
            return pltpu.make_async_copy(home(n), mine(n), get_sem.at[n])

        def hand(n):
            return remote(home(n), mine(n), hsend_sem.at[n], get_sem.at[n], peer)

        def leave(n):
            return remote(home(n, column), mine(n, column), hsend_sem.at[n], get_sem.at[n], goal)

        late_own = functools.reduce(jnp.logical_or, [me == n for n in LATE_OWN])
        late_peer = me == LATE_PEER

        def send_now(n):
            @pl.when(here)
            def _():
                stay(n).start()

            @pl.when(beside)
            def _():
                hand(n).start()

            @pl.when(away)
            def _():
                leave(n).start()

        def send_home(n):
            @pl.when(jnp.logical_not(jnp.logical_or(late_own, late_peer)))
            def _():
                send_now(n)

        loads[4].wait()
        send_home(0)
        sent_to, row = 0, 0
        jobs = [(0, raw_qkv), (1, raw_o), (2, raw_up)]
        jobs += [(3, raw_down.at[width * n : width * (n + 1)]) for n in range(raw_down.shape[0] // width)]
        ready = -1
        for load, src in jobs:
            if load > ready:
                loads[load].wait()
                ready = load
            for col in range(0, src.shape[1], width):
                turn(src.at[:, col : col + width], home_w, row)
                row += width
                while (sent_to + 1) * piece <= row:
                    sent_to += 1
                    send_home(sent_to)

        def to_x(n):
            return remote(mine(n, column), mine(n, column), send_sem.at[n, 0], put_sem.at[n, 0], next_x)

        def to_y(n):
            return remote(mine(n, column), mine(n, column), send_sem.at[n, 1], put_sem.at[n, 1], next_y)

        def on_y(n):
            return remote(mine(n, beside_x, 0), mine(n, beside_x, 0), send_sem.at[n, 2], put_sem.at[n, 2], next_y)

        def on_x(n):
            return remote(mine(n, beside_y, 1), mine(n, beside_y, 1), send_sem.at[n, 3], put_sem.at[n, 3], next_x)

        @pl.when(late_peer)
        def _():
            pl.semaphore_wait(late_sem, 1)
            for n in range(n_parts):
                send_now(n)

        @pl.when(is_local)
        def _():
            for n in range(n_parts):
                arrived(mine(n), get_sem.at[n])

        @pl.when(jnp.logical_not(is_local))
        def _():
            for n in range(n_parts + 2):
                if n < n_parts:
                    arrived(mine(n, column), get_sem.at[n])
                    to_x(n).start()
                    to_y(n).start()
                if 1 <= n <= n_parts:
                    arrived(mine(n - 1, beside_x), put_sem.at[n - 1, 0])
                    on_y(n - 1).start()
                    arrived(mine(n - 1, beside_y), put_sem.at[n - 1, 1])
                    on_x(n - 1).start()
                if n >= 2:
                    arrived(mine(n - 2, across, 0), put_sem.at[n - 2, 2])
                    arrived(mine(n - 2, across, 1), put_sem.at[n - 2, 3])

        @pl.when(late_own)
        def _():
            for n in range(n_parts):
                send_now(n)

        @pl.when(me == LATE_PEER - 1)
        def _():
            pl.semaphore_signal(late_sem, inc=1, device_id=peer, device_id_type=mesh_ids)

        loads[5].wait()
        turn(raw_skip.at[0:width], w_skip.at[0], 0)
        turn(raw_skip.at[width : 2 * width], w_skip.at[1], 0)
        for copy in warm:
            copy.wait()
        for s in range(samples):
            hub[s, 0] = raw_warm[0, s].T
            hub[s, SLOTS] = raw_warm[1, s].T
            x_t[s, 0] = x_ref[s]
        w_in[...] = jnp.zeros_like(w_in)
        w_in[:, 0 : win_ref.shape[0]] = win_ref[...].T

        t = Scratch()
        t.qkv, t.o, t.act, t.s, t.p = s_qkv, s_o, s_act, s_s, s_p
        steps_a, steps_b = steps - 1 - pair, steps - pair
        count = jnp.where(first_half, steps_a, steps_b)
        chained = jnp.where(first_half, pair > 0, pair < last_pair)
        chains = jnp.where(first_half, pair < last_pair, pair > 0)
        chain_count = jnp.where(first_half, steps - 3 - pair, steps_b)

        def chain(k, s):
            slot = lax.rem(k + 1, SLOTS)
            return remote(outs.at[s, lax.rem(k, 2)], hub.at[s, slot], csend_sem.at[s, lax.rem(k, 2)], crecv_sem.at[s, slot], chain_to)

        def skip(k, s):
            slot = lax.rem(k + 1, SLOTS)
            return remote(outs.at[s, lax.rem(k, 2)], hub.at[s, SLOTS + slot], ssend_sem.at[s, lax.rem(k, 2)], srecv_sem.at[s, slot], peer)

        def latent(k, s):
            slot = lax.rem(k + 1, 2)
            return remote(x_t.at[s, slot], x_t.at[s, slot], xsend_sem.at[s, slot], xrecv_sem.at[s, slot], peer)

        def tell(n, s):
            return remote(x_end.at[s], x_end.at[s], esend_sem.at[s, n], erecv_sem.at[s], {"data": group, "stage": n})

        def mods_at(k):
            return all_mod[pl.ds(pl.multiple_of(k * mod_rows, 8), mod_rows)]

        for half in range(2):
            spread(mods_at(0), half, mod_b.at[0])

        def step(m, _):
            k, s = m // samples, lax.rem(m, samples)
            slot, at = lax.rem(k, SLOTS), lax.rem(k, 2)

            @pl.when(jnp.logical_and(k > 0, chained))
            def _():
                arrived(hub.at[s, slot], crecv_sem.at[s, slot])

            @pl.when(jnp.logical_and(first_half, pair == 0))
            def _():
                @pl.when(k > 0)
                def _():
                    arrived(x_t.at[s, at], xrecv_sem.at[s, at])

                fill = jnp.zeros((CHUNK - channels, x_t.shape[3]), BF16)
                x_pad = jnp.concatenate([x_t[s, at].astype(BF16), fill], axis=0)
                for row in range(0, width, CHUNK):
                    h_ref[row : row + CHUNK] = product(w_in[row : row + CHUNK], x_pad)

            @pl.when(jnp.logical_and(first_half, pair > 0))
            def _():
                h_ref[...] = hub[s, slot].astype(F32)

            @pl.when(second_half)
            def _():
                @pl.when(k > 0)
                def _():
                    arrived(hub.at[s, SLOTS + slot], srecv_sem.at[s, slot])

                main = jnp.where(jnp.logical_and(k > 0, pair == last_pair), SLOTS + slot, slot)
                for row in range(0, width, CHUNK):
                    rows = slice(row, row + CHUNK)
                    h_ref[rows] = product(w_skip[1, rows], hub[s, SLOTS + slot]) + product(w_skip[0, rows], hub[s, main])

                @pl.when(k + SLOTS < count)
                def _():
                    pl.semaphore_signal(scredit_sem.at[s], inc=1, device_id=peer, device_id_type=mesh_ids)

            @pl.when(jnp.logical_and(chained, k + SLOTS < count))
            def _():
                pl.semaphore_signal(ccredit_sem.at[s], inc=1, device_id=chain_from, device_id_type=mesh_ids)

            @pl.when(k > 1)
            def _():
                @pl.when(first_half)
                def _():
                    skip(k - 2, s).wait_send()

                @pl.when(chains)
                def _():
                    chain(k - 2, s).wait_send()

            block(
                h_ref, mod_b.at[at], all_w, outs.at[s, at], t, heads,
                lambda: spread(mods_at(jnp.minimum(k + 1, steps - 1)), s, mod_b.at[1 - at]),
            )

            @pl.when(jnp.logical_and(chains, k < chain_count))
            def _():
                @pl.when(k + 1 >= SLOTS)
                def _():
                    pl.semaphore_wait(ccredit_sem.at[s], 1)

                chain(k, s).start()

            @pl.when(first_half)
            def _():
                @pl.when(k + 1 >= SLOTS)
                def _():
                    pl.semaphore_wait(scredit_sem.at[s], 1)

                skip(k, s).start()

            @pl.when(jnp.logical_and(second_half, pair == 0))
            def _():
                @pl.when(k > 1)
                def _():
                    latent(k - 2, s).wait_send()

                noise = product(wout_ref[...], outs[s, at])
                x_new = keep_ref[k] * x_t[s, at] + noise_ref[k] * noise
                x_t[s, 1 - at] = x_new

                @pl.when(k < steps - 2)
                def _():
                    latent(k, s).start()

                @pl.when(k == steps - 1)
                def _():
                    x_end[s] = x_new
                    for n in range(stages):

                        @pl.when(n != me)
                        def _():
                            tell(n, s).start()

            return 0

        lax.fori_loop(0, count * samples, step, 0)

        for s in range(samples):
            for back in (2, 1):

                @pl.when(first_half)
                def _():
                    skip(count - back, s).wait_send()

                @pl.when(jnp.logical_and(second_half, chains))
                def _():
                    chain(count - back, s).wait_send()

        for n in range(n_parts):

            @pl.when(beside)
            def _():
                hand(n).wait_send()

            @pl.when(away)
            def _():
                leave(n).wait_send()

            @pl.when(jnp.logical_not(is_local))
            def _():
                for copy in (to_x(n), to_y(n), on_y(n), on_x(n)):
                    copy.wait_send()

        holder = jnp.logical_and(second_half, pair == 0)
        for s in range(samples):

            @pl.when(holder)
            def _():
                for n in range(stages):

                    @pl.when(n != me)
                    def _():
                        tell(n, s).wait_send()

            @pl.when(jnp.logical_not(holder))
            def _():
                arrived(x_end.at[s], erecv_sem.at[s])

            out_ref[s] = x_end[s]

    def local_run(x_init, h_warm, skip_warm, w_in, w_out, w_qkv, w_o, w_up, w_down, w_skip, ada_mods, keep, noise):
        batch, tokens, channels = x_init.shape
        width, ff = w_up.shape[1], w_up.shape[2]
        heads = w_o.shape[1]
        steps = ada_mods.shape[0]
        rows = 4 * width + 2 * ff
        mod_rows = 6 * width // 128
        any_ = pl.BlockSpec(memory_space=pl.ANY)
        vmem = pl.BlockSpec(memory_space=pltpu.VMEM)
        smem = pl.BlockSpec(memory_space=pltpu.SMEM)
        V = pltpu.VMEM
        D = pltpu.SemaphoreType.DMA
        R = pltpu.SemaphoreType.REGULAR
        parts = PIECES + 1
        scratch = [
            V((width, 3 * width), BF16), V((width, width), BF16), V((width, ff), BF16), V((ff, width), BF16),
            V((rows, width), BF16), V((steps * mod_rows, 128), F32), V((rows, width), BF16), V((steps * mod_rows, 128), F32),
            V((2 * width, width), BF16), V((2, width, width), BF16), V((2, batch, tokens, width), BF16), V((width, CHUNK), BF16),
            V((batch, 2 * SLOTS, width, tokens), BF16), V((batch, 2, width, tokens), BF16),
            V((batch, 2, channels, tokens), F32), V((batch, channels, tokens), F32), V((width, tokens), F32),
            V((3 * width, tokens), BF16), V((width, tokens), BF16), V((ff, tokens), BF16),
            V((AHEAD + 1, tokens, tokens), F32), V((2, tokens, tokens), BF16), V((2, 6, width, 128), F32),
            D((6,)), D((2,)), D((parts,)), D((parts,)), D((parts, 4)), D((parts, 4)),
            D((batch, 2)), D((batch, SLOTS)), D((batch, 2)), D((batch, SLOTS)), D((batch, 2)), D((batch, 2)),
            D((batch, stages)), D((batch,)), R, R((batch,)), R((batch,)),
        ]
        call = pl.pallas_call(
            functools.partial(kernel, steps, heads),
            out_shape=jax.ShapeDtypeStruct((batch, channels, tokens), F32),
            in_specs=[vmem, any_, any_, vmem, vmem, any_, any_, any_, any_, any_, any_, smem, smem],
            out_specs=vmem,
            scratch_shapes=scratch,
            compiler_params=pltpu.CompilerParams(has_side_effects=True, vmem_limit_bytes=60 * 2**20),
            name="staged_sampler",
        )
        made = call(
            x_init.swapaxes(1, 2), h_warm, skip_warm, w_in, w_out.T, w_qkv, w_o.reshape(1, width, width), w_up, w_down,
            w_skip, ada_mods.reshape(steps * mod_rows, 128), keep, noise,
        )
        return made.swapaxes(1, 2)

    in_specs = (P('data'), P(None, 'data'), P(None, 'data'), P(), P(), P('stage'), P('stage'), P('stage'), P('stage'), P(), P(None, 'stage'), P(), P())
    return jax.shard_map(local_run, mesh=mesh, in_specs=in_specs, out_specs=P('data'), check_vma=False)
```

time: 1640 us -> 411 us (0.25)
  matrix products: 507 us -> 0 us
  waiting for transfers between devices: 426 us -> 0 us
  Pallas kernels: 0 us -> 409 us
  starting transfers between devices: 365 us -> 0 us
  other arithmetic: 182 us -> 0 us
  local copies, waits for them, and re-layouts: 99.4 us -> 1.38 us
  blocking collectives: 45 us -> 0 us
    dot_general x192 -> x0, matrix products: 507 us -> none  [the longest x32 176 us: value_a9(): jnp.einsum('btf,fd->btd', gelu_act, wdown_one, preferred_element_type=jnp...]
    ppermute x96 -> x0, waiting for transfers between devices: 426 us -> none  [the longest x32 426 us: step_body(): next_skips = lax.ppermute(jnp.stack(block_outs), 'stage', mirror_perm)]
    pallas_call x0 -> x1, Pallas kernels: none -> 409 us  [local_run(): call(x_init.swapaxes(1, 2), h_warm, skip_warm, w_in, w_out.T, w_qkv, w_o....]
    ppermute x96 -> x0, starting transfers between devices: 365 us -> none  [the longest x32 278 us: step_body(): next_skips = lax.ppermute(jnp.stack(block_outs), 'stage', mirror_perm)]
    sub x32 -> x0, other arithmetic: 95.3 us -> none  [value_a9(): attn_probs = jax.nn.softmax(scores, axis=-1).astype(jnp.bfloat16)]
    reduce_sum x96 -> x0, other arithmetic: 60.5 us -> none  [the longest x64 55.7 us: layer_norm(): variance = jnp.mean(centered * centered, axis=-1, keepdims=True)]
    convert_element_type x32 -> x0, local copies, waits for them, and re-layouts: 54.4 us -> none  [value_a9(): jnp.einsum('btd,de->bte', normed.astype(jnp.bfloat16), wqkv_one, preferre...]
    psum x1 -> x0, blocking collectives: 45 us -> none  [local_run(): lax.psum(jnp.where(stage_id == stages - 1, final_latent, jnp.zeros_like(f...]
  transfers between devices with their start and end apart: 96 -> 0, of which waited for: 32 -> 0; matrix products, arithmetic and copies ran while one was open for 5% -> 0% of each run, Pallas kernels for 0% -> 0%
where the time goes in v3:
time: 411 us
  Pallas kernels  409 us (100%)
    pallas_call x1, Pallas kernels, local_run(): call(x_init.swapaxes(1, 2), h_warm, skip_warm, w_in, w_out.T, w_qkv, w_o....  409 us

profile of v3, /device:TPU:21, one launch (start us, length us, event | category | flops | bytes accessed | tf_op | source)
XLA Modules:
  0.0 410.5 jit_solution(6322558949731219193)
XLA Ops:
  0.0 409.1 %staged_sampler.1 = f32[2,16,256]{2,1,0:T(8,128)} custom-call(f32[2,16,256]{2,1,0:T(8,128)} %bitcast.8, bf16[15,2,256,512]{3,2,1,0:T(8,128)(2,1)} %hwarm_ref.1, bf16[8,2,256,512]{3,2,1,0:T(8,128)(2,1)} %swarm_ref.1, bf16[16,512]{1,0:T(8,128)(2,1)} %win_ref.1, bf16[16,512]{1,0:T(8,128)(2,1)} %bitcast.9, bf16[1,512,1536]{2,1,0:T(8,128)(2,1)} %wqkv_ref.1, ...), custom_call_target="tpu_custom_call" | custom-call | tf_op jit(solution)/shard_map/staged_sampler/pallas_call | solution.py:543
  409.2 1.4 copy.15

commit v4 on v3

--- a/solution.py
+++ b/solution.py
@@ -14,8 +14,7 @@
 CORES = 2
 COLUMNS = 4
 PIECES = 6
-LATE_OWN = (8, 9)
-LATE_PEER = 3
+FIRST = 1
 SLOTS = 4
 EPS = 1e-6
 AHEAD = 3
@@ -144,12 +143,12 @@
         hub, outs, x_t, x_end, h_ref, s_qkv, s_o, s_act, s_s, s_p, mod_b,
         load_sem, warm_sem, hsend_sem, get_sem, send_sem, put_sem,
         csend_sem, crecv_sem, ssend_sem, srecv_sem, xsend_sem, xrecv_sem, esend_sem, erecv_sem,
-        late_sem, ccredit_sem, scredit_sem,
+        ccredit_sem, scredit_sem,
     ):
         me = lax.axis_index("stage")
         group = lax.axis_index("data")
         chip, core = me // CORES, lax.rem(me, CORES)
-        pair = lax.rem(chips - chip, chips)
+        pair = lax.rem(chips + FIRST - chip, chips)
         first_half, second_half = core == 0, core == 1
         stage = jnp.where(first_half, pair, stages - 1 - pair)
         last_pair = chips - 1
@@ -180,6 +179,14 @@
 
         def arrived(ref, sem):
             pltpu.make_async_copy(ref, ref, sem).wait()
+
+        barrier = pltpu.get_barrier_semaphore()
+        for n in range(1, stages):
+            pl.semaphore_signal(
+                barrier, inc=1, device_id={"data": group, "stage": lax.rem(me + n, stages)}, device_id_type=mesh_ids
+            )
+        for beyond in (next_x, next_y):
+            pl.semaphore_signal(barrier, inc=1, device_id=beyond, device_id_type=mesh_ids)
 
         raws = [raw_qkv, raw_o, raw_up, raw_down]
         homes = [wqkv_ref, wo_ref, wup_ref, wdown_ref]
@@ -201,7 +208,7 @@
                 dst[row + at : row + at + CHUNK, :] = src[:, at : at + CHUNK].T
 
         home_pair = jnp.minimum(me, stages - 1 - me)
-        goal_chip, goal_core = lax.rem(chips - home_pair, chips), jnp.where(me < chips, 0, 1)
+        goal_chip, goal_core = lax.rem(chips + FIRST - home_pair, chips), jnp.where(me < chips, 0, 1)
         goal = device(goal_chip, goal_core)
         here = jnp.logical_and(goal_chip == chip, goal_core == core)
         beside = jnp.logical_and(goal_chip == chip, goal_core != core)
@@ -209,34 +216,36 @@
         is_local = stage // CORES == chip
         piece = home_w.shape[0] // PIECES
 
-        def part(n, ref_w, ref_mod, column_=None, half=None):
+        def part(n, ref_w, ref_mod, column_=None, third=None):
             size, at = (ref_mod.shape[0], 0) if n == 0 else (piece, (n - 1) * piece)
             if column_ is not None:
                 size //= COLUMNS
                 at = at + column_ * size
-            if half is not None:
-                size //= 2
-                at = at + half * size
+            if third is not None:
+                unit = 8 if n == 0 else 16
+                least = size // (3 * unit) * unit
+                size, shift = [(size - 2 * least, 0), (least, size - 2 * least), (least, size - least)][third]
+                at = at + shift
             rows = pl.ds(at if isinstance(at, int) else pl.multiple_of(at, 8 if n == 0 else 16), size)
             return (ref_mod if n == 0 else ref_w).at[rows]
 
-        def home(n, column_=None):
-            return part(n, home_w, home_mod, column_)
-
-        def mine(n, column_=None, half=None):
-            return part(n, all_w, all_mod, column_, half)
+        def home(n, column_=None, third=None):
+            return part(n, home_w, home_mod, column_, third)
+
+        def mine(n, column_=None, third=None):
+            return part(n, all_w, all_mod, column_, third)
 
         def stay(n):
-            return pltpu.make_async_copy(home(n), mine(n), get_sem.at[n])
+            return pltpu.make_async_copy(home(n), mine(n), get_sem.at[n, 0])
 
         def hand(n):
-            return remote(home(n), mine(n), hsend_sem.at[n], get_sem.at[n], peer)
+            return remote(home(n), mine(n), hsend_sem.at[n, 0], get_sem.at[n, 0], peer)
 
         def leave(n):
-            return remote(home(n, column), mine(n, column), hsend_sem.at[n], get_sem.at[n], goal)
-
-        late_own = functools.reduce(jnp.logical_or, [me == n for n in LATE_OWN])
-        late_peer = me == LATE_PEER
+            return remote(home(n, column), mine(n, column), hsend_sem.at[n, 0], get_sem.at[n, 0], goal)
+
+        def leave_more(n):
+            return remote(home(n, across, 0), mine(n, across, 0), hsend_sem.at[n, 1], get_sem.at[n, 1], goal)
 
         def send_now(n):
             @pl.when(here)
@@ -250,15 +259,10 @@
             @pl.when(away)
             def _():
                 leave(n).start()
-
-        def send_home(n):
-            @pl.when(jnp.logical_not(jnp.logical_or(late_own, late_peer)))
-            def _():
-                send_now(n)
+                leave_more(n).start()
 
         loads[4].wait()
-        send_home(0)
-        sent_to, row = 0, 0
+        sent, row = -1, 0
         jobs = [(0, raw_qkv), (1, raw_o), (2, raw_up)]
         jobs += [(3, raw_down.at[width * n : width * (n + 1)]) for n in range(raw_down.shape[0] // width)]
         ready = -1
@@ -269,9 +273,11 @@
             for col in range(0, src.shape[1], width):
                 turn(src.at[:, col : col + width], home_w, row)
                 row += width
-                while (sent_to + 1) * piece <= row:
-                    sent_to += 1
-                    send_home(sent_to)
+                while (sent + 1) * piece <= row:
+                    if sent < 0:
+                        pl.semaphore_wait(barrier, stages + 1)
+                    sent += 1
+                    send_now(sent)
 
         def to_x(n):
             return remote(mine(n, column), mine(n, column), send_sem.at[n, 0], put_sem.at[n, 0], next_x)
@@ -280,27 +286,21 @@
             return remote(mine(n, column), mine(n, column), send_sem.at[n, 1], put_sem.at[n, 1], next_y)
 
         def on_y(n):
-            return remote(mine(n, beside_x, 0), mine(n, beside_x, 0), send_sem.at[n, 2], put_sem.at[n, 2], next_y)
+            return remote(mine(n, beside_x, 1), mine(n, beside_x, 1), send_sem.at[n, 2], put_sem.at[n, 2], next_y)
 
         def on_x(n):
-            return remote(mine(n, beside_y, 1), mine(n, beside_y, 1), send_sem.at[n, 3], put_sem.at[n, 3], next_x)
-
-        @pl.when(late_peer)
-        def _():
-            pl.semaphore_wait(late_sem, 1)
-            for n in range(n_parts):
-                send_now(n)
+            return remote(mine(n, beside_y, 2), mine(n, beside_y, 2), send_sem.at[n, 3], put_sem.at[n, 3], next_x)
 
         @pl.when(is_local)
         def _():
             for n in range(n_parts):
-                arrived(mine(n), get_sem.at[n])
+                arrived(mine(n), get_sem.at[n, 0])
 
         @pl.when(jnp.logical_not(is_local))
         def _():
             for n in range(n_parts + 2):
                 if n < n_parts:
-                    arrived(mine(n, column), get_sem.at[n])
+                    arrived(mine(n, column), get_sem.at[n, 0])
                     to_x(n).start()
                     to_y(n).start()
                 if 1 <= n <= n_parts:
@@ -309,17 +309,9 @@
                     arrived(mine(n - 1, beside_y), put_sem.at[n - 1, 1])
                     on_x(n - 1).start()
                 if n >= 2:
-                    arrived(mine(n - 2, across, 0), put_sem.at[n - 2, 2])
-                    arrived(mine(n - 2, across, 1), put_sem.at[n - 2, 3])
-
-        @pl.when(late_own)
-        def _():
-            for n in range(n_parts):
-                send_now(n)
-
-        @pl.when(me == LATE_PEER - 1)
-        def _():
-            pl.semaphore_signal(late_sem, inc=1, device_id=peer, device_id_type=mesh_ids)
+                    arrived(mine(n - 2, across, 0), get_sem.at[n - 2, 1])
+                    arrived(mine(n - 2, across, 1), put_sem.at[n - 2, 2])
+                    arrived(mine(n - 2, across, 2), put_sem.at[n - 2, 3])
 
         loads[5].wait()
         turn(raw_skip.at[0:width], w_skip.at[0], 0)
@@ -482,6 +474,7 @@
             @pl.when(away)
             def _():
                 leave(n).wait_send()
+                leave_more(n).wait_send()
 
             @pl.when(jnp.logical_not(is_local))
             def _():
@@ -527,9 +520,9 @@
             V((batch, 2, channels, tokens), F32), V((batch, channels, tokens), F32), V((width, tokens), F32),
             V((3 * width, tokens), BF16), V((width, tokens), BF16), V((ff, tokens), BF16),
             V((AHEAD + 1, tokens, tokens), F32), V((2, tokens, tokens), BF16), V((2, 6, width, 128), F32),
-            D((6,)), D((2,)), D((parts,)), D((parts,)), D((parts, 4)), D((parts, 4)),
+            D((6,)), D((2,)), D((parts, 2)), D((parts, 2)), D((parts, 4)), D((parts, 4)),
             D((batch, 2)), D((batch, SLOTS)), D((batch, 2)), D((batch, SLOTS)), D((batch, 2)), D((batch, 2)),
-            D((batch, stages)), D((batch,)), R, R((batch,)), R((batch,)),
+            D((batch, stages)), D((batch,)), R((batch,)), R((batch,)),
         ]
         call = pl.pallas_call(
             functools.partial(kernel, steps, heads),
@@ -537,7 +530,7 @@
             in_specs=[vmem, any_, any_, vmem, vmem, any_, any_, any_, any_, any_, any_, smem, smem],
             out_specs=vmem,
             scratch_shapes=scratch,
-            compiler_params=pltpu.CompilerParams(has_side_effects=True, vmem_limit_bytes=60 * 2**20),
+            compiler_params=pltpu.CompilerParams(collective_id=0, has_side_effects=True, vmem_limit_bytes=60 * 2**20),
             name="staged_sampler",
         )
         made = call(

time: 411 us -> 359 us (0.87)
  Pallas kernels: 409 us -> 358 us
    pallas_call x1, Pallas kernels: 409 us -> 358 us  [local_run(): call(x_init.swapaxes(1, 2), h_warm, skip_warm, w_in, w_out.T, w_qkv, w_o....]
where the time goes in v4:
time: 359 us
  Pallas kernels  358 us (100%)
    pallas_call x1, Pallas kernels, local_run(): call(x_init.swapaxes(1, 2), h_warm, skip_warm, w_in, w_out.T, w_qkv, w_o....  358 us

profile of v4, /device:TPU:21, one launch (start us, length us, event | category | flops | bytes accessed | tf_op | source)
XLA Modules:
  0.0 359.1 jit_solution(12256496417533894558)
XLA Ops:
  0.0 357.7 %staged_sampler.1 = f32[2,16,256]{2,1,0:T(8,128)} custom-call(f32[2,16,256]{2,1,0:T(8,128)} %bitcast.8, bf16[15,2,256,512]{3,2,1,0:T(8,128)(2,1)} %hwarm_ref.1, bf16[8,2,256,512]{3,2,1,0:T(8,128)(2,1)} %swarm_ref.1, bf16[16,512]{1,0:T(8,128)(2,1)} %win_ref.1, bf16[16,512]{1,0:T(8,128)(2,1)} %bitcast.9, bf16[1,512,1536]{2,1,0:T(8,128)(2,1)} %wqkv_ref.1, ...), custom_call_target="tpu_custom_call" | custom-call | tf_op jit(solution)/shard_map/staged_sampler/pallas_call | solution.py:536
  357.7 1.4 copy.15

commit v5 on v4

--- a/solution.py
+++ b/solution.py
@@ -13,11 +13,13 @@
 CHUNK = 256
 CORES = 2
 COLUMNS = 4
-PIECES = 6
+PIECES = (4, 8, 8, 8, 8, 7, 5)
 FIRST = 1
 SLOTS = 4
 EPS = 1e-6
-AHEAD = 3
+AHEAD = 5
+UP_AHEAD = 2
+DOWN_BEHIND = 1
 TANH_A = math.sqrt(2.0 / math.pi)
 TANH_B = TANH_A * 0.044715
 
@@ -26,12 +28,22 @@
     return jnp.dot(lhs, rhs, preferred_element_type=F32)
 
 
-def norm_mod(h, scale, shift):
-    width = h.shape[0]
-    mean = jnp.sum(h, axis=0, keepdims=True) * (1.0 / width)
-    c = h - mean
-    var = jnp.sum(c * c, axis=0, keepdims=True) * (1.0 / width)
-    return ((c * lax.rsqrt(var + EPS)) * scale + shift).astype(BF16)
+def norm_mod(h_ref, scale, shift):
+    width = h_ref.shape[0]
+
+    def total(term):
+        sums = [None] * 4
+        for n, row in enumerate(range(0, width, 8)):
+            v = term(h_ref[row : row + 8, :])
+            sums[n % 4] = v if sums[n % 4] is None else sums[n % 4] + v
+        return jnp.sum((sums[0] + sums[1]) + (sums[2] + sums[3]), axis=0, keepdims=True) * (1.0 / width)
+
+    mean = total(lambda v: v)
+    rate = lax.rsqrt(total(lambda v: (v - mean) * (v - mean)) + EPS)
+    rows = [slice(row, row + 16) for row in range(0, width, 16)]
+    return jnp.concatenate(
+        [(((h_ref[r, :] - mean) * rate) * wide(scale[r]) + wide(shift[r])).astype(BF16) for r in rows], axis=0
+    )
 
 
 def gelu(x):
@@ -41,7 +53,7 @@
 def softmax(s, scale):
     m = jnp.max(s, axis=0, keepdims=True)
     p = jnp.exp2((s - m) * (scale * math.log2(math.e)))
-    return (p * (1.0 / jnp.sum(p, axis=0, keepdims=True))).astype(BF16)
+    return p.astype(BF16), 1.0 / jnp.sum(p, axis=0, keepdims=True)
 
 
 def wide(cols):
@@ -69,27 +81,30 @@
     ff = (w.shape[0] - row_up) // 2
     row_down = row_up + ff
 
-    u = norm_mod(h_ref[...], wide(mod[1]), wide(mod[0]))
-    for row in (width, 0, 2 * width):
-        t.qkv[row : row + width] = product(w[row : row + width], u).astype(BF16)
+    u = norm_mod(h_ref, mod[1], mod[0])
+    for row, size in [(width + CHUNK * g, CHUNK) if n == 0 else (CHUNK * g, CHUNK) for g in range(groups) for n in range(2)] + [
+        (2 * width, width)
+    ]:
+        t.qkv[row : row + size] = product(w[row : row + size], u).astype(BF16)
 
     zero = jnp.zeros((dim, tokens), BF16)
-    keys = [t.qkv[width + CHUNK * g : width + CHUNK * (g + 1), :].T for g in range(groups)]
-    order = [g * per_group + j for j in range(per_group) for g in range(groups)]
-
-    def scores(n):
-        g, j = divmod(order[n], per_group)
-        query = t.qkv[dim * order[n] : dim * (order[n] + 1), :]
+    keys, rate = {}, {}
+
+    def scores(hd):
+        g, j = divmod(hd, per_group)
+        if g not in keys:
+            keys[g] = t.qkv[width + CHUNK * g : width + CHUNK * (g + 1), :].T
+        query = t.qkv[dim * hd : dim * (hd + 1), :]
         padded = jnp.concatenate([query if m == j else zero for m in range(per_group)], axis=0)
-        t.s[n % (AHEAD + 1)] = product(keys[g], padded)
-
-    def probs(n):
-        for c in range(0, tokens, 128):
-            t.p[n % 2, :, c : c + 128] = softmax(t.s[n % (AHEAD + 1), :, c : c + 128], 1.0 / math.sqrt(dim))
-
-    def values(n):
-        row = dim * order[n]
-        t.o[row : row + dim, :] = product(t.qkv[2 * width + row : 2 * width + row + dim, :], t.p[n % 2]).astype(BF16)
+        t.s[hd % (AHEAD + 1)] = product(keys[g], padded)
+
+    def probs(hd):
+        t.p[hd % 2], rate[hd] = softmax(t.s[hd % (AHEAD + 1)], 1.0 / math.sqrt(dim))
+
+    def values(hd):
+        row = dim * hd
+        v = product(t.qkv[2 * width + row : 2 * width + row + dim, :], t.p[hd % 2])
+        t.o[row : row + dim, :] = (v * rate[hd]).astype(BF16)
 
     for n in range(AHEAD):
         scores(n)
@@ -102,24 +117,35 @@
     for row in range(0, width, CHUNK):
         rows = slice(row, row + CHUNK)
         h_ref[rows] = h_ref[rows] + wide(mod[2, rows]) * product(w[row_o + row : row_o + row + CHUNK], t.o[...])
-    u = norm_mod(h_ref[...], wide(mod[4]), wide(mod[3]))
+    u = norm_mod(h_ref, mod[4], mod[3])
     chunks = ff // CHUNK
+    held, total = {}, [None] * (width // CHUNK)
 
     def up(n):
-        return product(w[row_up + CHUNK * n : row_up + CHUNK * (n + 1)], u)
-
-    held, total = up(0), None
+        held[n] = product(w[row_up + CHUNK * n : row_up + CHUNK * (n + 1)], u)
+
+    def down(n):
+        at, col = divmod(CHUNK * n, width)
+        for q in range(len(total)):
+            row = row_down + width * at + CHUNK * q
+            part = product(w[row : row + CHUNK, col : col + CHUNK], t.act[CHUNK * n : CHUNK * (n + 1), :])
+            total[q] = part if total[q] is None else total[q] + part
+
+    for n in range(UP_AHEAD):
+        up(n)
     for n in range(chunks):
-        ahead = up(n + 1) if n + 1 < chunks else None
-        rows = slice(CHUNK * n, CHUNK * (n + 1))
-        t.act[rows, :] = gelu(held)
-        held = ahead
+        if n + UP_AHEAD < chunks:
+            up(n + UP_AHEAD)
+        t.act[CHUNK * n : CHUNK * (n + 1), :] = gelu(held.pop(n))
         if n == 0:
             extra()
-        at, col = divmod(CHUNK * n, width)
-        part = product(w[row_down + width * at : row_down + width * (at + 1), col : col + CHUNK], t.act[rows, :])
-        total = part if total is None else total + part
-    out[...] = (h_ref[...] + wide(mod[5]) * total).astype(BF16)
+        if n >= DOWN_BEHIND:
+            down(n - DOWN_BEHIND)
+    for n in range(chunks - DOWN_BEHIND, chunks):
+        down(n)
+    for q, v in enumerate(total):
+        rows = slice(CHUNK * q, CHUNK * (q + 1))
+        out[rows] = (h_ref[rows] + wide(mod[5, rows]) * v).astype(BF16)
 
 
 class Scratch:
@@ -154,7 +180,7 @@
         last_pair = chips - 1
         samples, channels = x_ref.shape[0], x_ref.shape[1]
         width = raw_o.shape[0]
-        n_parts = PIECES + 1
+        n_parts = len(PIECES) + 1
         mod_rows = 6 * width // 128
         mesh_ids = pl.DeviceIdType.MESH
 
@@ -214,38 +240,35 @@
         beside = jnp.logical_and(goal_chip == chip, goal_core != core)
         away = goal_chip != chip
         is_local = stage // CORES == chip
-        piece = home_w.shape[0] // PIECES
-
-        def part(n, ref_w, ref_mod, column_=None, third=None):
-            size, at = (ref_mod.shape[0], 0) if n == 0 else (piece, (n - 1) * piece)
+        shared = n_parts - 1
+        ends = [home_w.shape[0] * sum(PIECES[:n]) // sum(PIECES) for n in range(n_parts)]
+
+        def part(n, ref_w, ref_mod, column_=None, half=None):
+            size, at = (ref_mod.shape[0], 0) if n == 0 else (ends[n] - ends[n - 1], ends[n - 1])
             if column_ is not None:
                 size //= COLUMNS
                 at = at + column_ * size
-            if third is not None:
-                unit = 8 if n == 0 else 16
-                least = size // (3 * unit) * unit
-                size, shift = [(size - 2 * least, 0), (least, size - 2 * least), (least, size - least)][third]
-                at = at + shift
+            if half is not None:
+                size //= 2
+                at = at + half * size
             rows = pl.ds(at if isinstance(at, int) else pl.multiple_of(at, 8 if n == 0 else 16), size)
             return (ref_mod if n == 0 else ref_w).at[rows]
 
-        def home(n, column_=None, third=None):
-            return part(n, home_w, home_mod, column_, third)
-
-        def mine(n, column_=None, third=None):
-            return part(n, all_w, all_mod, column_, third)
+        def home(n, column_=None):
+            return part(n, home_w, home_mod, column_)
+
+        def mine(n, column_=None, half=None):
+            return part(n, all_w, all_mod, column_, half)
 
         def stay(n):
-            return pltpu.make_async_copy(home(n), mine(n), get_sem.at[n, 0])
+            return pltpu.make_async_copy(home(n), mine(n), get_sem.at[n])
 
         def hand(n):
-            return remote(home(n), mine(n), hsend_sem.at[n, 0], get_sem.at[n, 0], peer)
+            return remote(home(n), mine(n), hsend_sem.at[n], get_sem.at[n], peer)
 
         def leave(n):
-            return remote(home(n, column), mine(n, column), hsend_sem.at[n, 0], get_sem.at[n, 0], goal)
-
-        def leave_more(n):
-            return remote(home(n, across, 0), mine(n, across, 0), hsend_sem.at[n, 1], get_sem.at[n, 1], goal)
+            which = column if n < shared else None
+            return remote(home(n, which), mine(n, which), hsend_sem.at[n], get_sem.at[n], goal)
 
         def send_now(n):
             @pl.when(here)
@@ -259,7 +282,6 @@
             @pl.when(away)
             def _():
                 leave(n).start()
-                leave_more(n).start()
 
         loads[4].wait()
         sent, row = -1, 0
@@ -273,7 +295,7 @@
             for col in range(0, src.shape[1], width):
                 turn(src.at[:, col : col + width], home_w, row)
                 row += width
-                while (sent + 1) * piece <= row:
+                while sent + 1 < n_parts and ends[sent + 1] <= row:
                     if sent < 0:
                         pl.semaphore_wait(barrier, stages + 1)
                     sent += 1
@@ -286,32 +308,33 @@
             return remote(mine(n, column), mine(n, column), send_sem.at[n, 1], put_sem.at[n, 1], next_y)
 
         def on_y(n):
-            return remote(mine(n, beside_x, 1), mine(n, beside_x, 1), send_sem.at[n, 2], put_sem.at[n, 2], next_y)
+            return remote(mine(n, beside_x, 0), mine(n, beside_x, 0), send_sem.at[n, 2], put_sem.at[n, 2], next_y)
 
         def on_x(n):
-            return remote(mine(n, beside_y, 2), mine(n, beside_y, 2), send_sem.at[n, 3], put_sem.at[n, 3], next_x)
+            return remote(mine(n, beside_y, 1), mine(n, beside_y, 1), send_sem.at[n, 3], put_sem.at[n, 3], next_x)
 
         @pl.when(is_local)
         def _():
             for n in range(n_parts):
-                arrived(mine(n), get_sem.at[n, 0])
+                arrived(mine(n), get_sem.at[n])
 
         @pl.when(jnp.logical_not(is_local))
         def _():
-            for n in range(n_parts + 2):
-                if n < n_parts:
-                    arrived(mine(n, column), get_sem.at[n, 0])
+            for n in range(shared + 2):
+                if n < shared:
+                    arrived(mine(n, column), get_sem.at[n])
                     to_x(n).start()
                     to_y(n).start()
-                if 1 <= n <= n_parts:
+                if 1 <= n <= shared:
                     arrived(mine(n - 1, beside_x), put_sem.at[n - 1, 0])
                     on_y(n - 1).start()
                     arrived(mine(n - 1, beside_y), put_sem.at[n - 1, 1])
                     on_x(n - 1).start()
                 if n >= 2:
-                    arrived(mine(n - 2, across, 0), get_sem.at[n - 2, 1])
-                    arrived(mine(n - 2, across, 1), put_sem.at[n - 2, 2])
-                    arrived(mine(n - 2, across, 2), put_sem.at[n - 2, 3])
+                    arrived(mine(n - 2, across, 0), put_sem.at[n - 2, 2])
+                    arrived(mine(n - 2, across, 1), put_sem.at[n - 2, 3])
+            for n in range(shared, n_parts):
+                arrived(mine(n), get_sem.at[n])
 
         loads[5].wait()
         turn(raw_skip.at[0:width], w_skip.at[0], 0)
@@ -474,12 +497,13 @@
             @pl.when(away)
             def _():
                 leave(n).wait_send()
-                leave_more(n).wait_send()
-
-            @pl.when(jnp.logical_not(is_local))
-            def _():
-                for copy in (to_x(n), to_y(n), on_y(n), on_x(n)):
-                    copy.wait_send()
+
+            if n < shared:
+
+                @pl.when(jnp.logical_not(is_local))
+                def _():
+                    for copy in (to_x(n), to_y(n), on_y(n), on_x(n)):
+                        copy.wait_send()
 
         holder = jnp.logical_and(second_half, pair == 0)
         for s in range(samples):
@@ -511,7 +535,7 @@
         V = pltpu.VMEM
         D = pltpu.SemaphoreType.DMA
         R = pltpu.SemaphoreType.REGULAR
-        parts = PIECES + 1
+        parts = len(PIECES) + 1
         scratch = [
             V((width, 3 * width), BF16), V((width, width), BF16), V((width, ff), BF16), V((ff, width), BF16),
             V((rows, width), BF16), V((steps * mod_rows, 128), F32), V((rows, width), BF16), V((steps * mod_rows, 128), F32),
@@ -520,7 +544,7 @@
             V((batch, 2, channels, tokens), F32), V((batch, channels, tokens), F32), V((width, tokens), F32),
             V((3 * width, tokens), BF16), V((width, tokens), BF16), V((ff, tokens), BF16),
             V((AHEAD + 1, tokens, tokens), F32), V((2, tokens, tokens), BF16), V((2, 6, width, 128), F32),
-            D((6,)), D((2,)), D((parts, 2)), D((parts, 2)), D((parts, 4)), D((parts, 4)),
+            D((6,)), D((2,)), D((parts,)), D((parts,)), D((parts, 4)), D((parts, 4)),
             D((batch, 2)), D((batch, SLOTS)), D((batch, 2)), D((batch, SLOTS)), D((batch, 2)), D((batch, 2)),
             D((batch, stages)), D((batch,)), R((batch,)), R((batch,)),
         ]

time: 359 us -> 331 us (0.922)
  Pallas kernels: 358 us -> 330 us
    pallas_call x1, Pallas kernels: 358 us -> 330 us  [local_run(): call(x_init.swapaxes(1, 2), h_warm, skip_warm, w_in, w_out.T, w_qkv, w_o....]
where the time goes in v5:
time: 331 us
  Pallas kernels  330 us (100%)
    pallas_call x1, Pallas kernels, local_run(): call(x_init.swapaxes(1, 2), h_warm, skip_warm, w_in, w_out.T, w_qkv, w_o....  330 us

profile of v5, /device:TPU:21, one launch (start us, length us, event | category | flops | bytes accessed | tf_op | source)
XLA Modules:
  0.0 330.9 jit_solution(312969494733699349)
XLA Ops:
  0.0 329.6 %staged_sampler.1 = f32[2,16,256]{2,1,0:T(8,128)} custom-call(f32[2,16,256]{2,1,0:T(8,128)} %bitcast.8, bf16[15,2,256,512]{3,2,1,0:T(8,128)(2,1)} %hwarm_ref.1, bf16[8,2,256,512]{3,2,1,0:T(8,128)(2,1)} %swarm_ref.1, bf16[16,512]{1,0:T(8,128)(2,1)} %win_ref.1, bf16[16,512]{1,0:T(8,128)(2,1)} %bitcast.9, bf16[1,512,1536]{2,1,0:T(8,128)(2,1)} %wqkv_ref.1, ...), custom_call_target="tpu_custom_call" | custom-call | tf_op jit(solution)/shard_map/staged_sampler/pallas_call | solution.py:560
  329.6 1.4 copy.15

commit v6 on v5

--- a/solution.py
+++ b/solution.py
@@ -13,6 +13,7 @@
 CHUNK = 256
 CORES = 2
 COLUMNS = 4
+HEAD = 8
 PIECES = (4, 8, 8, 8, 8, 7, 5)
 FIRST = 1
 SLOTS = 4
@@ -180,7 +181,7 @@
         last_pair = chips - 1
         samples, channels = x_ref.shape[0], x_ref.shape[1]
         width = raw_o.shape[0]
-        n_parts = len(PIECES) + 1
+        n_parts = len(PIECES) + 2
         mod_rows = 6 * width // 128
         mesh_ids = pl.DeviceIdType.MESH
 
@@ -240,19 +241,24 @@
         beside = jnp.logical_and(goal_chip == chip, goal_core != core)
         away = goal_chip != chip
         is_local = stage // CORES == chip
-        shared = n_parts - 1
-        ends = [home_w.shape[0] * sum(PIECES[:n]) // sum(PIECES) for n in range(n_parts)]
+        shared, tail = n_parts - 2, n_parts - 1
+        ends = [home_w.shape[0] * sum(PIECES[:n]) // sum(PIECES) for n in range(tail)]
+        head_rows = HEAD * mod_rows
 
         def part(n, ref_w, ref_mod, column_=None, half=None):
-            size, at = (ref_mod.shape[0], 0) if n == 0 else (ends[n] - ends[n - 1], ends[n - 1])
+            is_mod = n in (0, tail)
+            if is_mod:
+                size, at = (head_rows, 0) if n == 0 else (ref_mod.shape[0] - head_rows, head_rows)
+            else:
+                size, at = ends[n] - ends[n - 1], ends[n - 1]
             if column_ is not None:
                 size //= COLUMNS
                 at = at + column_ * size
             if half is not None:
                 size //= 2
                 at = at + half * size
-            rows = pl.ds(at if isinstance(at, int) else pl.multiple_of(at, 8 if n == 0 else 16), size)
-            return (ref_mod if n == 0 else ref_w).at[rows]
+            rows = pl.ds(at if isinstance(at, int) else pl.multiple_of(at, 8 if is_mod else 16), size)
+            return (ref_mod if is_mod else ref_w).at[rows]
 
         def home(n, column_=None):
             return part(n, home_w, home_mod, column_)
@@ -295,11 +301,12 @@
             for col in range(0, src.shape[1], width):
                 turn(src.at[:, col : col + width], home_w, row)
                 row += width
-                while sent + 1 < n_parts and ends[sent + 1] <= row:
+                while sent + 1 < tail and ends[sent + 1] <= row:
                     if sent < 0:
                         pl.semaphore_wait(barrier, stages + 1)
                     sent += 1
                     send_now(sent)
+        send_now(tail)
 
         def to_x(n):
             return remote(mine(n, column), mine(n, column), send_sem.at[n, 0], put_sem.at[n, 0], next_x)
@@ -313,9 +320,29 @@
         def on_x(n):
             return remote(mine(n, beside_y, 1), mine(n, beside_y, 1), send_sem.at[n, 3], put_sem.at[n, 3], next_x)
 
+        def mods_at(k):
+            return all_mod[pl.ds(pl.multiple_of(k * mod_rows, 8), mod_rows)]
+
+        def prepare():
+            loads[5].wait()
+            turn(raw_skip.at[0:width], w_skip.at[0], 0)
+            turn(raw_skip.at[width : 2 * width], w_skip.at[1], 0)
+            for copy in warm:
+                copy.wait()
+            for s in range(samples):
+                hub[s, 0] = raw_warm[0, s].T
+                hub[s, SLOTS] = raw_warm[1, s].T
+                x_t[s, 0] = x_ref[s]
+            w_in[...] = jnp.zeros_like(w_in)
+            w_in[:, 0 : win_ref.shape[0]] = win_ref[...].T
+            for half in range(2):
+                spread(mods_at(0), half, mod_b.at[0])
+
         @pl.when(is_local)
         def _():
-            for n in range(n_parts):
+            arrived(mine(0), get_sem.at[0])
+            prepare()
+            for n in range(1, tail):
                 arrived(mine(n), get_sem.at[n])
 
         @pl.when(jnp.logical_not(is_local))
@@ -333,20 +360,10 @@
                 if n >= 2:
                     arrived(mine(n - 2, across, 0), put_sem.at[n - 2, 2])
                     arrived(mine(n - 2, across, 1), put_sem.at[n - 2, 3])
-            for n in range(shared, n_parts):
+                if n == 2:
+                    prepare()
+            for n in range(shared, tail):
                 arrived(mine(n), get_sem.at[n])
-
-        loads[5].wait()
-        turn(raw_skip.at[0:width], w_skip.at[0], 0)
-        turn(raw_skip.at[width : 2 * width], w_skip.at[1], 0)
-        for copy in warm:
-            copy.wait()
-        for s in range(samples):
-            hub[s, 0] = raw_warm[0, s].T
-            hub[s, SLOTS] = raw_warm[1, s].T
-            x_t[s, 0] = x_ref[s]
-        w_in[...] = jnp.zeros_like(w_in)
-        w_in[:, 0 : win_ref.shape[0]] = win_ref[...].T
 
         t = Scratch()
         t.qkv, t.o, t.act, t.s, t.p = s_qkv, s_o, s_act, s_s, s_p
@@ -371,15 +388,13 @@
         def tell(n, s):
             return remote(x_end.at[s], x_end.at[s], esend_sem.at[s, n], erecv_sem.at[s], {"data": group, "stage": n})
 
-        def mods_at(k):
-            return all_mod[pl.ds(pl.multiple_of(k * mod_rows, 8), mod_rows)]
-
-        for half in range(2):
-            spread(mods_at(0), half, mod_b.at[0])
-
         def step(m, _):
             k, s = m // samples, lax.rem(m, samples)
             slot, at = lax.rem(k, SLOTS), lax.rem(k, 2)
+
+            @pl.when(m == HEAD // 2 * samples)
+            def _():
+                arrived(mine(tail), get_sem.at[tail])
 
             @pl.when(jnp.logical_and(k > 0, chained))
             def _():
@@ -535,7 +550,7 @@
         V = pltpu.VMEM
         D = pltpu.SemaphoreType.DMA
         R = pltpu.SemaphoreType.REGULAR
-        parts = len(PIECES) + 1
+        parts = len(PIECES) + 2
         scratch = [
             V((width, 3 * width), BF16), V((width, width), BF16), V((width, ff), BF16), V((ff, width), BF16),
             V((rows, width), BF16), V((steps * mod_rows, 128), F32), V((rows, width), BF16), V((steps * mod_rows, 128), F32),

time: 331 us -> 328 us (level)
  no operation moved by 1% of the time
where the time goes in v6:
time: 328 us
  Pallas kernels  327 us (100%)
    pallas_call x1, Pallas kernels, local_run(): call(x_init.swapaxes(1, 2), h_warm, skip_warm, w_in, w_out.T, w_qkv, w_o....  327 us

profile of v6, /device:TPU:21, one launch (start us, length us, event | category | flops | bytes accessed | tf_op | source)
XLA Modules:
  0.0 328.2 jit_solution(17358035453454948205)
XLA Ops:
  0.0 326.8 %staged_sampler.1 = f32[2,16,256]{2,1,0:T(8,128)} custom-call(f32[2,16,256]{2,1,0:T(8,128)} %bitcast.8, bf16[15,2,256,512]{3,2,1,0:T(8,128)(2,1)} %hwarm_ref.1, bf16[8,2,256,512]{3,2,1,0:T(8,128)(2,1)} %swarm_ref.1, bf16[16,512]{1,0:T(8,128)(2,1)} %win_ref.1, bf16[16,512]{1,0:T(8,128)(2,1)} %bitcast.9, bf16[1,512,1536]{2,1,0:T(8,128)(2,1)} %wqkv_ref.1, ...), custom_call_target="tpu_custom_call" | custom-call | tf_op jit(solution)/shard_map/staged_sampler/pallas_call | solution.py:575
  326.8 1.4 copy.15

commit v7 on v6

--- a/solution.py
+++ b/solution.py
@@ -396,6 +396,16 @@
             def _():
                 arrived(mine(tail), get_sem.at[tail])
 
+            @pl.when(k > 1)
+            def _():
+                @pl.when(first_half)
+                def _():
+                    skip(k - 2, s).wait_send()
+
+                @pl.when(chains)
+                def _():
+                    chain(k - 2, s).wait_send()
+
             @pl.when(jnp.logical_and(k > 0, chained))
             def _():
                 arrived(hub.at[s, slot], crecv_sem.at[s, slot])
@@ -426,24 +436,6 @@
                     rows = slice(row, row + CHUNK)
                     h_ref[rows] = product(w_skip[1, rows], hub[s, SLOTS + slot]) + product(w_skip[0, rows], hub[s, main])
 
-                @pl.when(k + SLOTS < count)
-                def _():
-                    pl.semaphore_signal(scredit_sem.at[s], inc=1, device_id=peer, device_id_type=mesh_ids)
-
-            @pl.when(jnp.logical_and(chained, k + SLOTS < count))
-            def _():
-                pl.semaphore_signal(ccredit_sem.at[s], inc=1, device_id=chain_from, device_id_type=mesh_ids)
-
-            @pl.when(k > 1)
-            def _():
-                @pl.when(first_half)
-                def _():
-                    skip(k - 2, s).wait_send()
-
-                @pl.when(chains)
-                def _():
-                    chain(k - 2, s).wait_send()
-
             block(
                 h_ref, mod_b.at[at], all_w, outs.at[s, at], t, heads,
                 lambda: spread(mods_at(jnp.minimum(k + 1, steps - 1)), s, mod_b.at[1 - at]),
@@ -464,6 +456,14 @@
                     pl.semaphore_wait(scredit_sem.at[s], 1)
 
                 skip(k, s).start()
+
+            @pl.when(jnp.logical_and(second_half, k + SLOTS < count))
+            def _():
+                pl.semaphore_signal(scredit_sem.at[s], inc=1, device_id=peer, device_id_type=mesh_ids)
+
+            @pl.when(jnp.logical_and(chained, k + SLOTS < count))
+            def _():
+                pl.semaphore_signal(ccredit_sem.at[s], inc=1, device_id=chain_from, device_id_type=mesh_ids)
 
             @pl.when(jnp.logical_and(second_half, pair == 0))
             def _():

time: 328 us -> 328 us (level)
  no operation moved by 1% of the time
where the time goes in v7:
time: 328 us
  Pallas kernels  326 us (99%)
    pallas_call x1, Pallas kernels, local_run(): call(x_init.swapaxes(1, 2), h_warm, skip_warm, w_in, w_out.T, w_qkv, w_o....  326 us

profile of v7, /device:TPU:21, one launch (start us, length us, event | category | flops | bytes accessed | tf_op | source)
XLA Modules:
  0.0 327.7 jit_solution(4783448477571079240)
XLA Ops:
  0.0 326.3 %staged_sampler.1 = f32[2,16,256]{2,1,0:T(8,128)} custom-call(f32[2,16,256]{2,1,0:T(8,128)} %bitcast.8, bf16[15,2,256,512]{3,2,1,0:T(8,128)(2,1)} %hwarm_ref.1, bf16[8,2,256,512]{3,2,1,0:T(8,128)(2,1)} %swarm_ref.1, bf16[16,512]{1,0:T(8,128)(2,1)} %win_ref.1, bf16[16,512]{1,0:T(8,128)(2,1)} %bitcast.9, bf16[1,512,1536]{2,1,0:T(8,128)(2,1)} %wqkv_ref.1, ...), custom_call_target="tpu_custom_call" | custom-call | tf_op jit(solution)/shard_map/staged_sampler/pallas_call | solution.py:575
  326.3 1.4 copy.15
